TPU v7x, 256 devices: a whole 4x4x8 slice. The times are simulated.
256 devices in a mesh: grp: 8 (over z), pen: 32 (over y, x, core).
Axes of the slice: x: 4, y: 4, z: 8, core: 2. Of those that a mesh axis runs over, the one named last changes fastest.
Arguments:
- cell_offsets: int32 [2, 1048576], P(None, ('grp', 'pen')), may hold values from 0 to 1
- cell_z: int32 [1048576], P(('grp', 'pen')), may hold values from 0 to 255
- frac: float32 [3, 1048576], P(None, ('grp', 'pen')), may hold values from 0 to 1
- charges: float32 [1048576], P(('grp', 'pen')), may hold values from -4 to 4
- tile_counts: int32 [16384], P(('grp', 'pen')), may hold values from 16 to 64, as said below
Outputs:
- forces: float32 [3, 1048576], P(None, ('grp', 'pen'))
- energy: float32 [], replicated
Inputs may be any that keep to these rules, and one draw needn't show every extreme that they name: `tile_counts`: live slots of each tile; some tile holds 64.
All inputs are finite; a program needn't handle non-finite values.
Results may differ from a plain program's by a relative error of at most 0.0003.
Values sent between devices are 32-bit elements; how exact they have to be, the bound alone decides.
No kernel may reach another device: no remote copies, remote signals or barrier semaphores. Data moves between devices by JAX's collectives and lax.ppermute only.
A program may use at most 128 MiB of HBM per device.

v0:
```python
import functools
import math

import jax
import jax.numpy as jnp
import numpy as np
from jax import lax
from jax.experimental import pallas as pl
from jax.experimental.pallas import tpu as pltpu
from jax.sharding import PartitionSpec as P

K = 256
ATOMS = 1048576
EWALD_SPLIT = 0.6
AXES = ("grp", "pen")
N_GRP = 8
N_PEN = 32
BLOCK_X = K // N_GRP
BLOCK_Y = K // N_PEN
TILES_X = BLOCK_X // 2
PAD_X = BLOCK_X + 5
PAD_Y = BLOCK_Y + 5
USED = PAD_X * PAD_Y
CHUNK = 512
ROWS = 16 * (2 * TILES_X + 6)
ROW_X = 40
F32 = jnp.float32
BF16 = jnp.bfloat16


def halves(table):
    high = table.astype(np.float32).astype(jnp.bfloat16)
    low = (table - high.astype(np.float64)).astype(np.float32).astype(jnp.bfloat16)
    return high, low


def cas(rows, columns):
    angle = (np.outer(rows, columns) % K) * (2.0 * math.pi / K)
    return np.cos(angle) + np.sin(angle)


def make_tables():
    index = np.arange(K)
    full = cas(index, index)
    spread_y = (BLOCK_Y * np.arange(N_PEN)[None, :] + np.arange(16)[:, None]).reshape(-1)
    valid_y = np.repeat(np.arange(16) < PAD_Y, N_PEN)
    table_y = cas(spread_y, index) * valid_y[:, None]
    spread_x = (BLOCK_X * np.arange(N_GRP)[:, None] + np.arange(ROW_X)[None, :]).reshape(-1)
    valid_x = np.tile(np.arange(ROW_X) < PAD_X, N_GRP)
    table_x = cas(index, spread_x) * valid_x[None, :]
    frequency = np.where(2 * index < K, index, index - K) / K
    square = frequency * frequency
    coeffs = np.array([1.0, 26.0, 66.0, 26.0, 1.0]) / 120.0
    phase = np.exp(2j * math.pi * np.outer(index, np.arange(5)) / K)
    modulus = np.abs(phase @ coeffs) ** 2
    factor = np.exp(-(math.pi**2) * square / EWALD_SPLIT**2) / modulus
    plane_factor = np.outer(factor, factor) / (math.pi * float(K) ** 3)
    plane_square = square[:, None] + square[None, :]
    lone = np.stack([factor, square])
    return dict(
        full=halves(full),
        y=halves(table_y),
        x=halves(table_x),
        xt=halves(table_x.T),
        factor=plane_factor.astype(np.float32),
        square=plane_square.astype(np.float32),
        lone=lone.astype(np.float32),
    )


TABLES = make_tables()


def split(value):
    high = value.astype(BF16)
    low = (value - high.astype(F32)).astype(BF16)
    return high, low


def dot(left, right, dims=((1,), (0,))):
    return lax.dot_general(left, right, (dims, ((), ())), preferred_element_type=F32)


def dot3(left, right, dims=((1,), (0,))):
    return (
        dot(left[0], right[0], dims) + dot(left[1], right[0], dims) + dot(left[0], right[1], dims)
    )


def spline_rows(fracs):
    values = [jnp.ones_like(fracs)]
    fifth = values
    for order in range(2, 7):
        scale = 1.0 / (order - 1)
        nxt = []
        for j in range(order):
            term = None
            if j >= 1:
                term = values[j - 1] * ((fracs + float(order - 1 - j)) * scale)
            if j <= order - 2:
                part = values[j] * ((float(1 + j) - fracs) * scale)
                term = part if term is None else term + part
            nxt.append(term)
        if order == 5:
            fifth = nxt
        values = nxt
    slopes = []
    for j in range(6):
        if j == 0:
            slopes.append(-fifth[0])
        elif j == 5:
            slopes.append(fifth[4])
        else:
            slopes.append(fifth[j - 1] - fifth[j])
    return values, slopes


def iota(shape, axis):
    return lax.broadcasted_iota(jnp.int32, shape, axis)


def pick(distance, rows):
    value = jnp.zeros(distance.shape, F32)
    for j in range(6):
        value = jnp.where(distance == j, rows[j], value)
    return value


def column_parts(column, counts_ref, offsets_ref, cell_z_ref, frac_ref, charges_ref):
    lanes = pl.ds(pl.multiple_of(column * 256, 256), 256)
    values, slopes = spline_rows(frac_ref[:, lanes])
    lane = iota((1, 256), 1)
    tile = lane // 64
    counts = jnp.full((1, 256), counts_ref[4 * column], jnp.int32)
    for b in range(1, 4):
        counts = jnp.where(tile == b, counts_ref[4 * column + b], counts)
    live_q = jnp.where(lane % 64 < counts, charges_ref[:, lanes], 0.0)
    rows = [[value[d : d + 1, :] for value in values] for d in range(3)]
    grades = [[slope[d : d + 1, :] for slope in slopes] for d in range(3)]
    from_x = iota((8, 256), 0) - offsets_ref[0:1, lanes]
    from_y = iota((16, 256), 0) - (offsets_ref[1:2, lanes] + 2 * tile)
    from_z = (iota((256, 256), 0) - cell_z_ref[:, lanes]) & (K - 1)
    return lanes, live_q, rows, grades, from_x, from_y, from_z


def spread_kernel(
    counts_ref, offsets_ref, cell_z_ref, frac_ref, charges_ref, high_ref, low_ref, out_ref,
    mesh_ref, packed_ref,
):
    mesh_ref[...] = jnp.zeros_like(mesh_ref)

    @pl.loop(0, TILES_X)
    def _(column):
        lanes, live_q, rows, grades, from_x, from_y, from_z = column_parts(
            column, counts_ref, offsets_ref, cell_z_ref, frac_ref, charges_ref
        )
        weight_x = pick(from_x, rows[0]) * live_q
        weight_y = pick(from_y, rows[1])
        pair = jnp.concatenate([weight_x[i : i + 1, :] * weight_y for i in range(8)], axis=0)
        weight_z = pick(from_z, rows[2])
        part = dot3(split(pair), split(weight_z), ((1,), (1,)))
        place = pl.ds(pl.multiple_of(column * 32, 32), 128)
        for h in range(2):
            mesh_ref[h, place, :] += part[:, 128 * h : 128 * h + 128]

    for y in range(PAD_Y):
        for h in range(2):
            packed_ref[PAD_X * y : PAD_X * (y + 1), 128 * h : 128 * h + 128] = mesh_ref[
                h, pl.ds(y, PAD_X, stride=16), :
            ]
    packed_ref[USED:, :] = jnp.zeros((CHUNK - USED, 256), F32)
    spectrum = dot3((high_ref[...], low_ref[...]), split(packed_ref[...]), ((1,), (1,)))
    for j in range(4):
        out_ref[pl.ds(j, 256, stride=4), :] = spectrum[:, 128 * j : 128 * j + 128]


def plane_kernel(
    lone_ref, in_ref, factor_ref, square_ref, yh_ref, yl_ref, xh_ref, xl_ref, xth_ref, xtl_ref,
    out_ref, turned_ref, wide_ref,
):
    for j in range(4):
        turned = in_ref[pl.ds(j, 256, stride=4), :].T
        for h in range(2):
            turned_ref[h, 128 * j : 128 * j + 128, :] = turned[:, 128 * h : 128 * h + 128]
    section = iota((ROW_X, 128), 1) // 32
    for g in range(N_GRP):
        for quad in range(4):
            block = jnp.zeros((ROW_X, 128), F32)
            for s in range(4):
                y = 4 * quad + s
                if y < PAD_Y:
                    piece = turned_ref[g // 4, PAD_X * y : PAD_X * y + ROW_X, :]
                    shift = (32 * (s - g % 4)) % 128
                    if shift:
                        piece = pltpu.roll(piece, shift, 1)
                    block = jnp.where(section == s, piece, block)
            wide_ref[ROW_X * g : ROW_X * (g + 1), 128 * quad : 128 * quad + 128] = block
    table_y = (yh_ref[...], yl_ref[...])
    half = dot3(split(wide_ref[...]), table_y)
    spectrum = dot3((xh_ref[...], xl_ref[...]), split(half))
    mode = lax.axis_index("grp") * N_PEN + lax.axis_index("pen")
    square = square_ref[...] + lone_ref[1, mode]
    nonzero = square > 0
    kernel = jnp.where(
        nonzero, factor_ref[...] * lone_ref[0, mode] / jnp.where(nonzero, square, 1.0), 0.0
    )
    scaled = kernel * spectrum
    energy = jnp.sum(jnp.sum(scaled * spectrum, axis=0, keepdims=True), axis=1, keepdims=True)
    energy = energy * (0.5 / ATOMS)
    back = dot3((xth_ref[...], xtl_ref[...]), split(scaled))
    wide_ref[...] = dot3(split(back), table_y, ((1,), (1,)))
    for y in range(PAD_Y):
        for h in range(2):
            block = jnp.zeros((ROW_X, 128), F32)
            for s in range(4):
                g = 4 * h + s
                piece = wide_ref[
                    ROW_X * g : ROW_X * (g + 1), 128 * (y // 4) : 128 * (y // 4) + 128
                ]
                shift = (32 * (s - y % 4)) % 128
                if shift:
                    piece = pltpu.roll(piece, shift, 1)
                block = jnp.where(section == s, piece, block)
            turned_ref[h, PAD_X * y : PAD_X * (y + 1), :] = block[:PAD_X]
    lane = iota((256, 128), 1)
    for h in range(2):
        turned_ref[h, USED:CHUNK, :] = jnp.zeros((CHUNK - USED, 128), F32)
    for j in range(4):
        rows = slice(128 * j, 128 * j + 128)
        block = jnp.concatenate([turned_ref[0, rows, :], turned_ref[1, rows, :]], axis=1).T
        if j == 3:
            block = jnp.where(lane == USED - 384, energy, block)
        out_ref[pl.ds(j, 256, stride=4), :] = block


def force_kernel(
    counts_ref, offsets_ref, cell_z_ref, frac_ref, charges_ref, in_ref, high_ref, low_ref,
    forces_ref, energy_ref, packed_ref, mesh_ref, mesh_high_ref, mesh_low_ref,
):
    table = (high_ref[...], low_ref[...])
    lane = iota((256, 128), 1)
    for j in range(4):
        chunk = in_ref[pl.ds(j, 256, stride=4), :]
        if j == 3:
            energies = jnp.where(lane == USED - 384, chunk, 0.0)
            energy_ref[...] = jnp.sum(
                jnp.sum(energies, axis=0, keepdims=True), axis=1, keepdims=True
            )
        packed_ref[128 * j : 128 * j + 128, :] = dot3(split(chunk.T), table)
    mesh_ref[...] = jnp.zeros_like(mesh_ref)
    for y in range(PAD_Y):
        for h in range(2):
            mesh_ref[h, pl.ds(y, PAD_X, stride=16), :] = packed_ref[
                PAD_X * y : PAD_X * (y + 1), 128 * h : 128 * h + 128
            ]
    for h in range(2):
        high, low = split(mesh_ref[h])
        mesh_high_ref[:, 128 * h : 128 * h + 128] = high
        mesh_low_ref[:, 128 * h : 128 * h + 128] = low

    @pl.loop(0, TILES_X)
    def _(column):
        lanes, live_q, rows, grades, from_x, from_y, from_z = column_parts(
            column, counts_ref, offsets_ref, cell_z_ref, frac_ref, charges_ref
        )
        weight_x = pick(from_x, rows[0])
        grade_x = pick(from_x, grades[0])
        weight_y = pick(from_y, rows[1])
        grade_y = pick(from_y, grades[1])
        place = pl.ds(pl.multiple_of(column * 32, 32), 128)
        footing = (mesh_high_ref[place, :], mesh_low_ref[place, :])
        main = dot3(footing, split(pick(from_z, rows[2])))
        tilt = dot3(footing, split(pick(from_z, grades[2])))
        along_x = 0.0
        along_y = 0.0
        along_z = 0.0
        for i in range(8):
            band = main[16 * i : 16 * i + 16, :]
            along_x = along_x + grade_x[i : i + 1, :] * band
            along_y = along_y + weight_x[i : i + 1, :] * band
            along_z = along_z + weight_x[i : i + 1, :] * tilt[16 * i : 16 * i + 16, :]
        forces_ref[0:1, lanes] = -live_q * jnp.sum(weight_y * along_x, axis=0, keepdims=True)
        forces_ref[1:2, lanes] = -live_q * jnp.sum(grade_y * along_y, axis=0, keepdims=True)
        forces_ref[2:3, lanes] = -live_q * jnp.sum(weight_y * along_z, axis=0, keepdims=True)


def call(kernel, out_shape, scratch, *args):
    specs = [
        pl.BlockSpec(memory_space=pltpu.SMEM if name == "s" else pltpu.VMEM) for name, _ in args
    ]
    vmem = pl.BlockSpec(memory_space=pltpu.VMEM)
    return pl.pallas_call(
        kernel,
        out_shape=out_shape,
        in_specs=specs,
        out_specs=jax.tree.map(lambda _: vmem, out_shape),
        scratch_shapes=scratch,
    )(*[value for _, value in args])


def exchange(block):
    return lax.all_to_all(block.reshape(256, 4, 128), AXES, 0, 0, tiled=True).reshape(1024, 128)


def local(cell_offsets, cell_z, frac, charges, tile_counts):
    slots = charges.shape[0]
    high, low = TABLES["full"]
    atoms = [
        ("s", tile_counts),
        ("v", cell_offsets),
        ("v", cell_z.reshape(1, slots)),
        ("v", frac),
        ("v", charges.reshape(1, slots)),
    ]
    table = [("v", jnp.asarray(high)), ("v", jnp.asarray(low))]
    block = jax.ShapeDtypeStruct((1024, 128), F32)
    outgoing = call(
        spread_kernel,
        block,
        [pltpu.VMEM((2, ROWS, 128), F32), pltpu.VMEM((CHUNK, 256), F32)],
        *atoms,
        *table,
    )
    plane = exchange(outgoing)
    planes = [TABLES["factor"], TABLES["square"], *TABLES["y"], *TABLES["x"], *TABLES["xt"]]
    returning = call(
        plane_kernel,
        block,
        [pltpu.VMEM((2, CHUNK, 128), F32), pltpu.VMEM((N_GRP * ROW_X, CHUNK), F32)],
        ("s", jnp.asarray(TABLES["lone"])),
        ("v", plane),
        *[("v", jnp.asarray(value)) for value in planes],
    )
    home = exchange(returning)
    forces, energy = call(
        force_kernel,
        (jax.ShapeDtypeStruct((3, slots), F32), jax.ShapeDtypeStruct((1, 1), F32)),
        [
            pltpu.VMEM((CHUNK, 256), F32),
            pltpu.VMEM((2, ROWS, 128), F32),
            pltpu.VMEM((ROWS, 256), BF16),
            pltpu.VMEM((ROWS, 256), BF16),
        ],
        *atoms,
        ("v", home),
        *table,
    )
    return forces, energy.reshape(())


def solution(mesh):
    return jax.shard_map(
        local,
        mesh=mesh,
        in_specs=(P(None, AXES), P(AXES), P(None, AXES), P(AXES), P(AXES)),
        out_specs=(P(None, AXES), P()),
        check_vma=False,
    )
```

profile of v0, /device:TPU:1, one launch (start us, length us, event | category | flops | bytes accessed | tf_op | source)
XLA Modules:
  0.0 87.8 jit_solution(7040031852706080543)
XLA Ops:
  0.6 8.7 %shard_map.167 = f32[1024,128]{1,0:T(8,128)} custom-call(s32[64]{0:T(128)} %counts_ref.3, s32[2,4096]{1,0:T(2,128)} %offsets_ref.3, s32[1,4096]{1,0:T(1,128)} %bitcast.11, f32[3,4096]{1,0:T(4,128)} %frac_ref.3, f32[1,4096]{1,0:T(1,128)} %bitcast.13, bf16[256,256]{1,0:T(8,128)(2,1)} %constant.22.clone.high_ref, bf16[256,256]{1,0:T(8,128)(2,1)} %constant.23.clone.low_ref), custom_call_target="tpu_custom_call" | custom-call | tf_op jit(solution)/shard_map/pallas_call | solution.py:292
  9.3 35.6 %all_to_all.10 = f32[256,4,128]{2,1,0:T(4,128)} all-to-all(f32[256,4,128]{2,1,0:T(4,128)} %bitcast.10), channel_id=1, replica_groups=mesh['grp'=8,'pen'=32] {'grp','pen'}, dimensions={0} | all-to-all | bytes 1048576 | tf_op jit(solution)/shard_map/all_to_all | solution.py:302
  44.9 5.3 %shard_map.168 = f32[1024,128]{1,0:T(8,128)} custom-call(f32[2,256]{1,0:T(2,128)} %constant.24.clone.lone_ref, f32[1024,128]{1,0:T(8,128)} %bitcast.7, f32[256,256]{1,0:T(8,128)} %constant.25.clone.factor_ref, f32[256,256]{1,0:T(8,128)} %constant.26.clone.square_ref, bf16[512,256]{1,0:T(8,128)(2,1)} %constant.27.clone.yh_ref, ...), custom_call_target="tpu_custom_call" | custom-call | tf_op jit(solution)/shard_map/pallas_call | solution.py:292
  50.3 27.2 %all_to_all.11 = f32[256,4,128]{2,1,0:T(4,128)} all-to-all(f32[256,4,128]{2,1,0:T(4,128)} %bitcast.8), channel_id=1, replica_groups=mesh['grp'=8,'pen'=32] {'grp','pen'}, dimensions={0} | all-to-all | bytes 1048576 | tf_op jit(solution)/shard_map/all_to_all | solution.py:302
  77.5 10.4 %shard_map.169 = (f32[3,4096]{1,0:T(4,128)}, f32[1,1]{1,0:T(1,128)}) custom-call(s32[64]{0:T(128)} %counts_ref.3, s32[2,4096]{1,0:T(2,128)} %offsets_ref.3, s32[1,4096]{1,0:T(1,128)} %bitcast.12, f32[3,4096]{1,0:T(4,128)} %frac_ref.3, f32[1,4096]{1,0:T(1,128)} %bitcast.14, f32[1024,128]{1,0:T(8,128)} %bitcast.9, bf16[256,256]{1,0:T(8,128)(2,1)} %constant.22.clone.high_ref, ...), custom_call_target="tpu_custom_call" | custom-call | tf_op jit(solution)/shard_map/pallas_call | solution.py:292
where the time goes:
time: 88.1 us; the launch traced here: 87.8 us
  blocking collectives  62.8 us (71%)
  Pallas kernels  24.3 us (28%)
    all_to_all x2, blocking collectives, exchange(): lax.all_to_all(block.reshape(256, 4, 128), AXES, 0, 0, tiled=True)  62.8 us
    pallas_call x3, Pallas kernels, call(): pl.pallas_call(kernel, out_shape=out_shape, in_specs=specs, out_specs=jax...  24.3 us

commit v1 on v0

--- a/solution.py
+++ b/solution.py
@@ -139,8 +139,19 @@
     grades = [[slope[d : d + 1, :] for slope in slopes] for d in range(3)]
     from_x = iota((8, 256), 0) - offsets_ref[0:1, lanes]
     from_y = iota((16, 256), 0) - (offsets_ref[1:2, lanes] + 2 * tile)
-    from_z = (iota((256, 256), 0) - cell_z_ref[:, lanes]) & (K - 1)
-    return lanes, live_q, rows, grades, from_x, from_y, from_z
+    cell_z = cell_z_ref[:, lanes]
+    from_z = (iota((16, 256), 0) - cell_z) & 15
+    owner_z = (((cell_z + from_z) & (K - 1)) >> 4).astype(F32).astype(BF16)
+    return lanes, live_q, rows, grades, from_x, from_y, from_z, owner_z
+
+
+def along_z(from_z, owner_z, rows):
+    zero = jnp.zeros((16, 256), BF16)
+    parts = split(pick(from_z, rows))
+    return tuple(
+        jnp.concatenate([jnp.where(owner_z == float(h), part, zero) for h in range(16)], axis=0)
+        for part in parts
+    )
 
 
 def spread_kernel(
@@ -149,16 +160,16 @@
 ):
     mesh_ref[...] = jnp.zeros_like(mesh_ref)
 
-    @pl.loop(0, TILES_X)
+    @pl.loop(0, TILES_X, unroll=4)
     def _(column):
-        lanes, live_q, rows, grades, from_x, from_y, from_z = column_parts(
+        lanes, live_q, rows, grades, from_x, from_y, from_z, owner_z = column_parts(
             column, counts_ref, offsets_ref, cell_z_ref, frac_ref, charges_ref
         )
         weight_x = pick(from_x, rows[0]) * live_q
         weight_y = pick(from_y, rows[1])
         pair = jnp.concatenate([weight_x[i : i + 1, :] * weight_y for i in range(8)], axis=0)
-        weight_z = pick(from_z, rows[2])
-        part = dot3(split(pair), split(weight_z), ((1,), (1,)))
+        weight_z = along_z(from_z, owner_z, rows[2])
+        part = dot3(split(pair), weight_z, ((1,), (1,)))
         place = pl.ds(pl.multiple_of(column * 32, 32), 128)
         for h in range(2):
             mesh_ref[h, place, :] += part[:, 128 * h : 128 * h + 128]
@@ -258,9 +269,9 @@
         mesh_high_ref[:, 128 * h : 128 * h + 128] = high
         mesh_low_ref[:, 128 * h : 128 * h + 128] = low
 
-    @pl.loop(0, TILES_X)
+    @pl.loop(0, TILES_X, unroll=4)
     def _(column):
-        lanes, live_q, rows, grades, from_x, from_y, from_z = column_parts(
+        lanes, live_q, rows, grades, from_x, from_y, from_z, owner_z = column_parts(
             column, counts_ref, offsets_ref, cell_z_ref, frac_ref, charges_ref
         )
         weight_x = pick(from_x, rows[0])
@@ -269,19 +280,19 @@
         grade_y = pick(from_y, grades[1])
         place = pl.ds(pl.multiple_of(column * 32, 32), 128)
         footing = (mesh_high_ref[place, :], mesh_low_ref[place, :])
-        main = dot3(footing, split(pick(from_z, rows[2])))
-        tilt = dot3(footing, split(pick(from_z, grades[2])))
-        along_x = 0.0
-        along_y = 0.0
-        along_z = 0.0
+        main = dot3(footing, along_z(from_z, owner_z, rows[2]))
+        tilt = dot3(footing, along_z(from_z, owner_z, grades[2]))
+        sum_x = 0.0
+        sum_y = 0.0
+        sum_z = 0.0
         for i in range(8):
             band = main[16 * i : 16 * i + 16, :]
-            along_x = along_x + grade_x[i : i + 1, :] * band
-            along_y = along_y + weight_x[i : i + 1, :] * band
-            along_z = along_z + weight_x[i : i + 1, :] * tilt[16 * i : 16 * i + 16, :]
-        forces_ref[0:1, lanes] = -live_q * jnp.sum(weight_y * along_x, axis=0, keepdims=True)
-        forces_ref[1:2, lanes] = -live_q * jnp.sum(grade_y * along_y, axis=0, keepdims=True)
-        forces_ref[2:3, lanes] = -live_q * jnp.sum(weight_y * along_z, axis=0, keepdims=True)
+            sum_x = sum_x + grade_x[i : i + 1, :] * band
+            sum_y = sum_y + weight_x[i : i + 1, :] * band
+            sum_z = sum_z + weight_x[i : i + 1, :] * tilt[16 * i : 16 * i + 16, :]
+        forces_ref[0:1, lanes] = -live_q * jnp.sum(weight_y * sum_x, axis=0, keepdims=True)
+        forces_ref[1:2, lanes] = -live_q * jnp.sum(grade_y * sum_y, axis=0, keepdims=True)
+        forces_ref[2:3, lanes] = -live_q * jnp.sum(weight_y * sum_z, axis=0, keepdims=True)
 
 
 def call(kernel, out_shape, scratch, *args):
@@ -295,6 +306,7 @@
         in_specs=specs,
         out_specs=jax.tree.map(lambda _: vmem, out_shape),
         scratch_shapes=scratch,
+        compiler_params=pltpu.CompilerParams(vmem_limit_bytes=16 * 1024 * 1024),
     )(*[value for _, value in args])
 
 

time: 88.1 us -> 80.3 us (0.911)
  Pallas kernels: 24.3 us -> 12.3 us
  local copies, waits for them, and re-layouts: 0 us -> 5.57 us
  blocking collectives: 62.8 us -> 61.2 us
    pallas_call x3, Pallas kernels: 24.3 us -> 12.3 us  [call(): pl.pallas_call(kernel, out_shape=out_shape, in_specs=specs, out_specs=jax...]
    unnamed x0 -> x44, local copies, waits for them, and re-layouts: none -> 5.57 us
    all_to_all x2, blocking collectives: 62.8 us -> 61.2 us  [exchange(): lax.all_to_all(block.reshape(256, 4, 128), AXES, 0, 0, tiled=True)]
where the time goes in v1:
time: 80.3 us; the launch traced here: 79.9 us
  blocking collectives  61.2 us (76%)
  Pallas kernels  12.3 us (15%)
  local copies, waits for them, and re-layouts  5.57 us (7%)
  between operations  0.83 us (1%)
    all_to_all x2, blocking collectives, exchange(): lax.all_to_all(block.reshape(256, 4, 128), AXES, 0, 0, tiled=True)  61.2 us
    pallas_call x3, Pallas kernels, call(): pl.pallas_call(kernel, out_shape=out_shape, in_specs=specs, out_specs=jax...  12.3 us
    unnamed x44, local copies, waits for them, and re-layouts  5.57 us

profile of v1, /device:TPU:1, one launch (start us, length us, event | category | flops | bytes accessed | tf_op | source)
XLA Modules:
  0.0 79.9 jit_solution(1946323217521359624)
XLA Ops:
  0.6 0.0 copy-start.21
  0.6 0.6 copy-done.21
  1.3 0.0 copy-start
  1.3 0.9 %copy-done = bf16[256,256]{1,0:T(8,128)(2,1)S(1)} copy-done((bf16[256,256]{1,0:T(8,128)(2,1)S(1)}, bf16[256,256]{1,0:T(8,128)(2,1)}, u32[]{:S(2)}) %copy-start) | copy-done | bytes 131096
  2.2 0.0 copy-start.2
  2.2 0.9 %copy-done.2 = bf16[256,256]{1,0:T(8,128)(2,1)S(1)} copy-done((bf16[256,256]{1,0:T(8,128)(2,1)S(1)}, bf16[256,256]{1,0:T(8,128)(2,1)}, u32[]{:S(2)}) %copy-start.2) | copy-done | bytes 131096
  3.1 0.0 copy-start.8
  3.1 0.8 %copy-done.8 = f32[3,4096]{1,0:T(4,128)S(1)} copy-done((f32[3,4096]{1,0:T(4,128)S(1)}, f32[3,4096]{1,0:T(4,128)}, u32[]{:S(2)}) %copy-start.8) | copy-done | bytes 49176
  3.9 0.0 copy-start.14
  3.9 0.8 copy-done.14
  4.7 0.0 copy-start.16
  4.7 0.7 copy-done.16
  5.4 0.0 copy-start.18
  5.4 0.7 copy-done.18
  6.1 0.0 copy-start.10
  6.1 0.0 copy-start.11
  6.1 0.0 copy-start.12
  6.1 0.0 copy-start.20
  6.2 4.0 %shard_map.167 = f32[1024,128]{1,0:T(8,128)S(1)} custom-call(s32[64]{0:T(128)S(1)} %copy-done.21, s32[2,4096]{1,0:T(2,128)S(1)} %copy-done.14, s32[1,4096]{1,0:T(1,128)S(1)} %bitcast.11, f32[3,4096]{1,0:T(4,128)S(1)} %copy-done.8, f32[1,4096]{1,0:T(1,128)S(1)} %bitcast.13, bf16[256,256]{1,0:T(8,128)(2,1)S(1)} %copy-done.2, bf16[256,256]{1,0:T(8,128)(2,1)S(1)} %copy-done), custom_call_target="tpu_custom_call" | custom-call | tf_op jit(solution)/shard_map/pallas_call | solution.py:303
  10.1 0.0 copy-start.4
  10.1 0.0 copy-start.5
  10.1 0.0 copy-start.6
  10.2 0.0 copy-start.7
  10.2 35.3 %all_to_all.10 = f32[256,4,128]{2,1,0:T(4,128)S(1)} all-to-all(f32[256,4,128]{2,1,0:T(4,128)S(1)} %bitcast.10), channel_id=1, replica_groups=mesh['grp'=8,'pen'=32] {'grp','pen'}, dimensions={0} | all-to-all | bytes 1048576 | tf_op jit(solution)/shard_map/all_to_all | solution.py:314
  45.5 0.0 copy-done.10
  45.5 0.0 copy-done.11
  45.5 0.0 copy-done.12
  45.5 0.0 copy-done.13
  45.5 0.0 copy-done.20
  45.5 0.0 copy-done.4
  45.5 0.0 copy-done.5
  45.6 0.0 copy-done.6
  45.6 0.0 copy-done.7
  45.6 3.5 %shard_map.168 = f32[1024,128]{1,0:T(8,128)S(1)} custom-call(f32[2,256]{1,0:T(2,128)S(1)} %copy-done.20, f32[1024,128]{1,0:T(8,128)S(1)} %bitcast.7, f32[256,256]{1,0:T(8,128)S(1)} %copy-done.7, f32[256,256]{1,0:T(8,128)S(1)} %copy-done.6, bf16[512,256]{1,0:T(8,128)(2,1)S(1)} %copy-done.5, bf16[512,256]{1,0:T(8,128)(2,1)S(1)} %copy-done.4, ...), custom_call_target="tpu_custom_call" | custom-call | tf_op jit(solution)/shard_map/pallas_call | solution.py:303
  49.1 0.0 copy-start.1
  49.1 0.0 copy-start.3
  49.1 0.0 copy-start.9
  49.1 0.0 copy-start.15
  49.2 0.0 copy-start.17
  49.2 0.0 copy-start.19
  49.2 25.9 %all_to_all.11 = f32[256,4,128]{2,1,0:T(4,128)S(1)} all-to-all(f32[256,4,128]{2,1,0:T(4,128)S(1)} %bitcast.8), channel_id=1, replica_groups=mesh['grp'=8,'pen'=32] {'grp','pen'}, dimensions={0} | all-to-all | bytes 1048576 | tf_op jit(solution)/shard_map/all_to_all | solution.py:314
  75.1 0.0 copy-done.1
  75.1 0.0 copy-done.3
  75.1 0.0 copy-done.9
  75.1 0.0 copy-done.15
  75.1 0.0 copy-done.17
  75.1 0.0 copy-done.19
  75.1 4.8 %shard_map.169 = (f32[3,4096]{1,0:T(4,128)}, f32[1,1]{1,0:T(1,128)}) custom-call(s32[64]{0:T(128)S(1)} %copy-done.21, s32[2,4096]{1,0:T(2,128)S(1)} %copy-done.15, s32[1,4096]{1,0:T(1,128)S(1)} %bitcast.12, f32[3,4096]{1,0:T(4,128)S(1)} %copy-done.9, f32[1,4096]{1,0:T(1,128)S(1)} %bitcast.14, f32[1024,128]{1,0:T(8,128)S(1)} %bitcast.9, ...), custom_call_target="tpu_custom_call" | custom-call | tf_op jit(solution)/shard_map/pallas_call | solution.py:303
  (1 shorter events, 0.0 us)
Async XLA Ops:
  0.6 0.7 copy-start.21
  1.3 0.9 %copy-start = (bf16[256,256]{1,0:T(8,128)(2,1)S(1)}, bf16[256,256]{1,0:T(8,128)(2,1)}, u32[]{:S(2)}) copy-start(bf16[256,256]{1,0:T(8,128)(2,1)} %constant.23.clone.low_ref) | copy-start | bytes 393220
  2.2 0.9 %copy-start.2 = (bf16[256,256]{1,0:T(8,128)(2,1)S(1)}, bf16[256,256]{1,0:T(8,128)(2,1)}, u32[]{:S(2)}) copy-start(bf16[256,256]{1,0:T(8,128)(2,1)} %constant.22.clone.high_ref) | copy-start | bytes 393220
  3.1 0.8 %copy-start.8 = (f32[3,4096]{1,0:T(4,128)S(1)}, f32[3,4096]{1,0:T(4,128)}, u32[]{:S(2)}) copy-start(f32[3,4096]{1,0:T(4,128)} %frac_ref.3) | copy-start | bytes 147460
  3.9 0.8 copy-start.14
  4.7 0.7 copy-start.16
  5.4 0.7 copy-start.18
  6.1 39.4 %copy-start.10 = (bf16[256,320]{1,0:T(8,128)(2,1)S(1)}, bf16[256,320]{1,0:T(8,128)(2,1)}, u32[]{:S(2)}) copy-start(bf16[256,320]{1,0:T(8,128)(2,1)} %constant.30.clone.xl_ref) | copy-start | bytes 491524
  6.1 39.4 %copy-start.11 = (bf16[256,320]{1,0:T(8,128)(2,1)S(1)}, bf16[256,320]{1,0:T(8,128)(2,1)}, u32[]{:S(2)}) copy-start(bf16[256,320]{1,0:T(8,128)(2,1)} %constant.29.clone.xh_ref) | copy-start | bytes 491524
  6.1 39.4 %copy-start.12 = (bf16[320,256]{1,0:T(8,128)(2,1)S(1)}, bf16[320,256]{1,0:T(8,128)(2,1)}, u32[]{:S(2)}) copy-start(bf16[320,256]{1,0:T(8,128)(2,1)} %constant.32.clone.xtl_ref) | copy-start | bytes 491524
  6.1 39.4 %copy-start.13 = (bf16[320,256]{1,0:T(8,128)(2,1)S(1)}, bf16[320,256]{1,0:T(8,128)(2,1)}, u32[]{:S(2)}) copy-start(bf16[320,256]{1,0:T(8,128)(2,1)} %constant.31.clone.xth_ref) | copy-start | bytes 491524
  6.1 39.4 %copy-start.20 = (f32[2,256]{1,0:T(2,128)S(1)}, f32[2,256]{1,0:T(2,128)}, u32[]{:S(2)}) copy-start(f32[2,256]{1,0:T(2,128)} %constant.24.clone.lone_ref) | copy-start | bytes 6148
  10.1 35.4 %copy-start.4 = (bf16[512,256]{1,0:T(8,128)(2,1)S(1)}, bf16[512,256]{1,0:T(8,128)(2,1)}, u32[]{:S(2)}) copy-start(bf16[512,256]{1,0:T(8,128)(2,1)} %constant.28.clone.yl_ref) | copy-start | bytes 786436
  10.1 35.4 %copy-start.5 = (bf16[512,256]{1,0:T(8,128)(2,1)S(1)}, bf16[512,256]{1,0:T(8,128)(2,1)}, u32[]{:S(2)}) copy-start(bf16[512,256]{1,0:T(8,128)(2,1)} %constant.27.clone.yh_ref) | copy-start | bytes 786436
  10.1 35.4 %copy-start.6 = (f32[256,256]{1,0:T(8,128)S(1)}, f32[256,256]{1,0:T(8,128)}, u32[]{:S(2)}) copy-start(f32[256,256]{1,0:T(8,128)} %constant.26.clone.square_ref) | copy-start | bytes 786436
  10.2 35.4 %copy-start.7 = (f32[256,256]{1,0:T(8,128)S(1)}, f32[256,256]{1,0:T(8,128)}, u32[]{:S(2)}) copy-start(f32[256,256]{1,0:T(8,128)} %constant.25.clone.factor_ref) | copy-start | bytes 786436
  49.1 26.0 %copy-start.1 = (bf16[256,256]{1,0:T(8,128)(2,1)S(1)}, bf16[256,256]{1,0:T(8,128)(2,1)}, u32[]{:S(2)}) copy-start(bf16[256,256]{1,0:T(8,128)(2,1)} %constant.23.clone.low_ref) | copy-start | bytes 393220
  49.1 25.9 %copy-start.3 = (bf16[256,256]{1,0:T(8,128)(2,1)S(1)}, bf16[256,256]{1,0:T(8,128)(2,1)}, u32[]{:S(2)}) copy-start(bf16[256,256]{1,0:T(8,128)(2,1)} %constant.22.clone.high_ref) | copy-start | bytes 393220
  49.1 25.9 %copy-start.9 = (f32[3,4096]{1,0:T(4,128)S(1)}, f32[3,4096]{1,0:T(4,128)}, u32[]{:S(2)}) copy-start(f32[3,4096]{1,0:T(4,128)} %frac_ref.3) | copy-start | bytes 147460
  49.1 25.9 %copy-start.15 = (s32[2,4096]{1,0:T(2,128)S(1)}, s32[2,4096]{1,0:T(2,128)}, u32[]{:S(2)}) copy-start(s32[2,4096]{1,0:T(2,128)} %offsets_ref.3) | copy-start | bytes 98308
  49.2 25.9 %copy-start.17 = (s32[4096]{0:T(1024)S(1)}, s32[4096]{0:T(1024)}, u32[]{:S(2)}) copy-start(s32[4096]{0:T(1024)} %param.17) | copy-start | bytes 49156
  49.2 25.9 %copy-start.19 = (f32[4096]{0:T(1024)S(1)}, f32[4096]{0:T(1024)}, u32[]{:S(2)}) copy-start(f32[4096]{0:T(1024)} %param.19) | copy-start | bytes 49156

commit v2 on v1

--- a/solution.py
+++ b/solution.py
@@ -24,6 +24,7 @@
 CHUNK = 512
 ROWS = 16 * (2 * TILES_X + 6)
 ROW_X = 40
+SPARE = 16
 F32 = jnp.float32
 BF16 = jnp.bfloat16
 
@@ -126,15 +127,10 @@
     return value
 
 
-def column_parts(column, counts_ref, offsets_ref, cell_z_ref, frac_ref, charges_ref):
+def column_parts(column, offsets_ref, cell_z_ref, frac_ref):
     lanes = pl.ds(pl.multiple_of(column * 256, 256), 256)
     values, slopes = spline_rows(frac_ref[:, lanes])
-    lane = iota((1, 256), 1)
-    tile = lane // 64
-    counts = jnp.full((1, 256), counts_ref[4 * column], jnp.int32)
-    for b in range(1, 4):
-        counts = jnp.where(tile == b, counts_ref[4 * column + b], counts)
-    live_q = jnp.where(lane % 64 < counts, charges_ref[:, lanes], 0.0)
+    tile = iota((1, 256), 1) // 64
     rows = [[value[d : d + 1, :] for value in values] for d in range(3)]
     grades = [[slope[d : d + 1, :] for slope in slopes] for d in range(3)]
     from_x = iota((8, 256), 0) - offsets_ref[0:1, lanes]
@@ -142,7 +138,7 @@
     cell_z = cell_z_ref[:, lanes]
     from_z = (iota((16, 256), 0) - cell_z) & 15
     owner_z = (((cell_z + from_z) & (K - 1)) >> 4).astype(F32).astype(BF16)
-    return lanes, live_q, rows, grades, from_x, from_y, from_z, owner_z
+    return lanes, rows, grades, from_x, from_y, from_z, owner_z
 
 
 def along_z(from_z, owner_z, rows):
@@ -155,31 +151,45 @@
 
 
 def spread_kernel(
-    counts_ref, offsets_ref, cell_z_ref, frac_ref, charges_ref, high_ref, low_ref, out_ref,
-    mesh_ref, packed_ref,
+    counts_hbm, offsets_hbm, cell_z_hbm, frac_hbm, charges_hbm, high_hbm, low_hbm, out_ref, live_ref,
+    mesh_ref, packed_ref, counts_ref, offsets_ref, cell_z_ref, frac_ref, charges_ref, high_ref,
+    low_ref, sems,
 ):
+    sources = [counts_hbm, offsets_hbm, cell_z_hbm, frac_hbm, charges_hbm, high_hbm, low_hbm]
+    targets = [counts_ref, offsets_ref, cell_z_ref, frac_ref, charges_ref, high_ref, low_ref]
+    copies = [
+        pltpu.make_async_copy(source, target, sems.at[i])
+        for i, (source, target) in enumerate(zip(sources, targets))
+    ]
+    for copy in copies:
+        copy.start()
     mesh_ref[...] = jnp.zeros_like(mesh_ref)
+    for copy in copies[:5]:
+        copy.wait()
 
     @pl.loop(0, TILES_X, unroll=4)
     def _(column):
-        lanes, live_q, rows, grades, from_x, from_y, from_z, owner_z = column_parts(
-            column, counts_ref, offsets_ref, cell_z_ref, frac_ref, charges_ref
+        lanes, rows, grades, from_x, from_y, from_z, owner_z = column_parts(
+            column, offsets_ref, cell_z_ref, frac_ref
         )
+        lane = iota((1, 256), 1)
+        counts = jnp.full((1, 256), counts_ref[4 * column], jnp.int32)
+        for b in range(1, 4):
+            counts = jnp.where(lane // 64 == b, counts_ref[4 * column + b], counts)
+        live_q = jnp.where(lane % 64 < counts, charges_ref[:, lanes], 0.0)
+        live_ref[:, lanes] = live_q
         weight_x = pick(from_x, rows[0]) * live_q
         weight_y = pick(from_y, rows[1])
         pair = jnp.concatenate([weight_x[i : i + 1, :] * weight_y for i in range(8)], axis=0)
         weight_z = along_z(from_z, owner_z, rows[2])
-        part = dot3(split(pair), weight_z, ((1,), (1,)))
         place = pl.ds(pl.multiple_of(column * 32, 32), 128)
-        for h in range(2):
-            mesh_ref[h, place, :] += part[:, 128 * h : 128 * h + 128]
-
-    for y in range(PAD_Y):
-        for h in range(2):
-            packed_ref[PAD_X * y : PAD_X * (y + 1), 128 * h : 128 * h + 128] = mesh_ref[
-                h, pl.ds(y, PAD_X, stride=16), :
-            ]
+        mesh_ref[place, :] += dot3(split(pair), weight_z, ((1,), (1,)))
+
+    for x in range(PAD_X):
+        packed_ref[PAD_Y * x : PAD_Y * (x + 1), :] = mesh_ref[16 * x : 16 * x + PAD_Y, :]
     packed_ref[USED:, :] = jnp.zeros((CHUNK - USED, 256), F32)
+    for copy in copies[5:]:
+        copy.wait()
     spectrum = dot3((high_ref[...], low_ref[...]), split(packed_ref[...]), ((1,), (1,)))
     for j in range(4):
         out_ref[pl.ds(j, 256, stride=4), :] = spectrum[:, 128 * j : 128 * j + 128]
@@ -193,6 +203,7 @@
         turned = in_ref[pl.ds(j, 256, stride=4), :].T
         for h in range(2):
             turned_ref[h, 128 * j : 128 * j + 128, :] = turned[:, 128 * h : 128 * h + 128]
+    turned_ref[:, CHUNK:, :] = jnp.zeros((2, SPARE, 128), F32)
     section = iota((ROW_X, 128), 1) // 32
     for g in range(N_GRP):
         for quad in range(4):
@@ -200,7 +211,7 @@
             for s in range(4):
                 y = 4 * quad + s
                 if y < PAD_Y:
-                    piece = turned_ref[g // 4, PAD_X * y : PAD_X * y + ROW_X, :]
+                    piece = turned_ref[g // 4, pl.ds(y, ROW_X, stride=PAD_Y), :]
                     shift = (32 * (s - g % 4)) % 128
                     if shift:
                         piece = pltpu.roll(piece, shift, 1)
@@ -210,10 +221,12 @@
     half = dot3(split(wide_ref[...]), table_y)
     spectrum = dot3((xh_ref[...], xl_ref[...]), split(half))
     mode = lax.axis_index("grp") * N_PEN + lax.axis_index("pen")
-    square = square_ref[...] + lone_ref[1, mode]
+    lone = jnp.where(iota((2, 256), 1) == mode, lone_ref[...], 0.0)
+    lone = jnp.sum(lone, axis=1, keepdims=True)
+    square = square_ref[...] + lone[1:2, :]
     nonzero = square > 0
     kernel = jnp.where(
-        nonzero, factor_ref[...] * lone_ref[0, mode] / jnp.where(nonzero, square, 1.0), 0.0
+        nonzero, factor_ref[...] * lone[0:1, :] / jnp.where(nonzero, square, 1.0), 0.0
     )
     scaled = kernel * spectrum
     energy = jnp.sum(jnp.sum(scaled * spectrum, axis=0, keepdims=True), axis=1, keepdims=True)
@@ -232,7 +245,7 @@
                 if shift:
                     piece = pltpu.roll(piece, shift, 1)
                 block = jnp.where(section == s, piece, block)
-            turned_ref[h, PAD_X * y : PAD_X * (y + 1), :] = block[:PAD_X]
+            turned_ref[h, pl.ds(y, PAD_X, stride=PAD_Y), :] = block[:PAD_X]
     lane = iota((256, 128), 1)
     for h in range(2):
         turned_ref[h, USED:CHUNK, :] = jnp.zeros((CHUNK - USED, 128), F32)
@@ -245,8 +258,8 @@
 
 
 def force_kernel(
-    counts_ref, offsets_ref, cell_z_ref, frac_ref, charges_ref, in_ref, high_ref, low_ref,
-    forces_ref, energy_ref, packed_ref, mesh_ref, mesh_high_ref, mesh_low_ref,
+    offsets_ref, cell_z_ref, frac_ref, live_ref, in_ref, high_ref, low_ref, forces_ref, energy_ref,
+    packed_ref, mesh_high_ref, mesh_low_ref,
 ):
     table = (high_ref[...], low_ref[...])
     lane = iota((256, 128), 1)
@@ -258,22 +271,19 @@
                 jnp.sum(energies, axis=0, keepdims=True), axis=1, keepdims=True
             )
         packed_ref[128 * j : 128 * j + 128, :] = dot3(split(chunk.T), table)
-    mesh_ref[...] = jnp.zeros_like(mesh_ref)
-    for y in range(PAD_Y):
-        for h in range(2):
-            mesh_ref[h, pl.ds(y, PAD_X, stride=16), :] = packed_ref[
-                PAD_X * y : PAD_X * (y + 1), 128 * h : 128 * h + 128
-            ]
-    for h in range(2):
-        high, low = split(mesh_ref[h])
-        mesh_high_ref[:, 128 * h : 128 * h + 128] = high
-        mesh_low_ref[:, 128 * h : 128 * h + 128] = low
+    for x in range(PAD_X):
+        high, low = split(packed_ref[PAD_Y * x : PAD_Y * x + 16, :])
+        mesh_high_ref[16 * x : 16 * x + 16, :] = high
+        mesh_low_ref[16 * x : 16 * x + 16, :] = low
+    mesh_high_ref[16 * PAD_X :, :] = jnp.zeros((ROWS - 16 * PAD_X, 256), BF16)
+    mesh_low_ref[16 * PAD_X :, :] = jnp.zeros((ROWS - 16 * PAD_X, 256), BF16)
 
     @pl.loop(0, TILES_X, unroll=4)
     def _(column):
-        lanes, live_q, rows, grades, from_x, from_y, from_z, owner_z = column_parts(
-            column, counts_ref, offsets_ref, cell_z_ref, frac_ref, charges_ref
+        lanes, rows, grades, from_x, from_y, from_z, owner_z = column_parts(
+            column, offsets_ref, cell_z_ref, frac_ref
         )
+        live_q = live_ref[:, lanes]
         weight_x = pick(from_x, rows[0])
         grade_x = pick(from_x, grades[0])
         weight_y = pick(from_y, rows[1])
@@ -295,19 +305,16 @@
         forces_ref[2:3, lanes] = -live_q * jnp.sum(weight_y * sum_z, axis=0, keepdims=True)
 
 
-def call(kernel, out_shape, scratch, *args):
-    specs = [
-        pl.BlockSpec(memory_space=pltpu.SMEM if name == "s" else pltpu.VMEM) for name, _ in args
-    ]
+def call(kernel, out_shape, scratch, *args, memory=pltpu.VMEM):
     vmem = pl.BlockSpec(memory_space=pltpu.VMEM)
     return pl.pallas_call(
         kernel,
         out_shape=out_shape,
-        in_specs=specs,
+        in_specs=[pl.BlockSpec(memory_space=memory)] * len(args),
         out_specs=jax.tree.map(lambda _: vmem, out_shape),
         scratch_shapes=scratch,
         compiler_params=pltpu.CompilerParams(vmem_limit_bytes=16 * 1024 * 1024),
-    )(*[value for _, value in args])
+    )(*args)
 
 
 def exchange(block):
@@ -316,32 +323,33 @@
 
 def local(cell_offsets, cell_z, frac, charges, tile_counts):
     slots = charges.shape[0]
-    high, low = TABLES["full"]
-    atoms = [
-        ("s", tile_counts),
-        ("v", cell_offsets),
-        ("v", cell_z.reshape(1, slots)),
-        ("v", frac),
-        ("v", charges.reshape(1, slots)),
-    ]
-    table = [("v", jnp.asarray(high)), ("v", jnp.asarray(low))]
+    cell_z = cell_z.reshape(1, slots)
+    charges = charges.reshape(1, slots)
+    table = [jnp.asarray(value) for value in TABLES["full"]]
     block = jax.ShapeDtypeStruct((1024, 128), F32)
-    outgoing = call(
+    sources = [tile_counts, cell_offsets, cell_z, frac, charges, *table]
+    outgoing, live_q = call(
         spread_kernel,
-        block,
-        [pltpu.VMEM((2, ROWS, 128), F32), pltpu.VMEM((CHUNK, 256), F32)],
-        *atoms,
-        *table,
+        (block, jax.ShapeDtypeStruct((1, slots), F32)),
+        [
+            pltpu.VMEM((ROWS, 256), F32),
+            pltpu.VMEM((CHUNK, 256), F32),
+            pltpu.SMEM(tile_counts.shape, jnp.int32),
+            *[pltpu.VMEM(source.shape, source.dtype) for source in sources[1:]],
+            pltpu.SemaphoreType.DMA((len(sources),)),
+        ],
+        *[pltpu.with_memory_space_constraint(source, pltpu.HBM) for source in sources],
+        memory=pltpu.HBM,
     )
     plane = exchange(outgoing)
     planes = [TABLES["factor"], TABLES["square"], *TABLES["y"], *TABLES["x"], *TABLES["xt"]]
     returning = call(
         plane_kernel,
         block,
-        [pltpu.VMEM((2, CHUNK, 128), F32), pltpu.VMEM((N_GRP * ROW_X, CHUNK), F32)],
-        ("s", jnp.asarray(TABLES["lone"])),
-        ("v", plane),
-        *[("v", jnp.asarray(value)) for value in planes],
+        [pltpu.VMEM((2, CHUNK + SPARE, 128), F32), pltpu.VMEM((N_GRP * ROW_X, CHUNK), F32)],
+        jnp.asarray(TABLES["lone"]),
+        plane,
+        *[jnp.asarray(value) for value in planes],
     )
     home = exchange(returning)
     forces, energy = call(
@@ -349,12 +357,14 @@
         (jax.ShapeDtypeStruct((3, slots), F32), jax.ShapeDtypeStruct((1, 1), F32)),
         [
             pltpu.VMEM((CHUNK, 256), F32),
-            pltpu.VMEM((2, ROWS, 128), F32),
             pltpu.VMEM((ROWS, 256), BF16),
             pltpu.VMEM((ROWS, 256), BF16),
         ],
-        *atoms,
-        ("v", home),
+        cell_offsets,
+        cell_z,
+        frac,
+        live_q,
+        home,
         *table,
     )
     return forces, energy.reshape(())

time: 80.3 us -> 75.2 us (0.936)
  local copies, waits for them, and re-layouts: 5.57 us -> 1.91 us
  Pallas kernels: 12.3 us -> 11.1 us
    unnamed x44 -> x28, local copies, waits for them, and re-layouts: 5.57 us -> 1.91 us
    pallas_call x3, Pallas kernels: 12.3 us -> 11.1 us  [call(): pl.pallas_call(kernel, out_shape=out_shape, in_specs=[pl.BlockSpec(memory...]
where the time goes in v2:
time: 75.2 us; the launch traced here: 75 us
  blocking collectives  61.2 us (81%)
  Pallas kernels  11.1 us (15%)
  local copies, waits for them, and re-layouts  1.91 us (3%)
  between operations  0.8 us (1%)
    all_to_all x2, blocking collectives, exchange(): lax.all_to_all(block.reshape(256, 4, 128), AXES, 0, 0, tiled=True)  61.2 us
    pallas_call x3, Pallas kernels, call(): pl.pallas_call(kernel, out_shape=out_shape, in_specs=[pl.BlockSpec(memory...  11.1 us
    unnamed x28, local copies, waits for them, and re-layouts  1.91 us

profile of v2, /device:TPU:1, one launch (start us, length us, event | category | flops | bytes accessed | tf_op | source)
XLA Modules:
  0.0 75.0 jit_solution(3976975302636288843)
XLA Ops:
  0.6 0.0 copy-start.7
  0.6 0.0 copy-start.8
  0.7 0.0 copy-start.13
  0.7 4.3 %shard_map.167 = (f32[1024,128]{1,0:T(8,128)S(1)}, f32[1,4096]{1,0:T(1,128)S(1)}) custom-call(s32[64]{0:T(128)} %counts_hbm.1, s32[2,4096]{1,0:T(2,128)} %offsets_ref.1, s32[1,4096]{1,0:T(1,128)} %bitcast.11, f32[3,4096]{1,0:T(4,128)} %frac_ref.1, f32[1,4096]{1,0:T(1,128)} %bitcast.13, bf16[256,256]{1,0:T(8,128)(2,1)} %constant.22.clone.high_hbm.high_ref, ...), custom_call_target="tpu_custom_call" | custom-call | tf_op jit(solution)/shard_map/pallas_call | solution.py:310
  5.0 0.0 copy-start.3
  5.0 0.0 copy-start.4
  5.0 0.0 copy-start.5
  5.1 0.0 copy-start.6
  5.1 35.3 %all_to_all.10 = f32[256,4,128]{2,1,0:T(4,128)S(1)} all-to-all(f32[256,4,128]{2,1,0:T(4,128)S(1)} %bitcast.10), channel_id=1, replica_groups=mesh['grp'=8,'pen'=32] {'grp','pen'}, dimensions={0} | all-to-all | bytes 1048576 | tf_op jit(solution)/shard_map/all_to_all | solution.py:321
  40.4 0.0 copy-done.7
  40.4 0.0 copy-done.8
  40.4 0.0 copy-done.13
  40.4 0.0 copy-done.3
  40.4 0.0 copy-done.4
  40.4 0.0 copy-done.5
  40.4 0.0 copy-done.6
  40.5 0.0 copy-start.9
  40.5 0.9 %copy-done.9 = bf16[320,256]{1,0:T(8,128)(2,1)S(1)} copy-done((bf16[320,256]{1,0:T(8,128)(2,1)S(1)}, bf16[320,256]{1,0:T(8,128)(2,1)}, u32[]{:S(2)}) %copy-start.9) | copy-done | bytes 163864
  41.4 0.0 copy-start.10
  41.4 0.9 %copy-done.10 = bf16[320,256]{1,0:T(8,128)(2,1)S(1)} copy-done((bf16[320,256]{1,0:T(8,128)(2,1)S(1)}, bf16[320,256]{1,0:T(8,128)(2,1)}, u32[]{:S(2)}) %copy-start.10) | copy-done | bytes 163864
  42.3 2.9 %shard_map.168 = f32[1024,128]{1,0:T(8,128)S(1)} custom-call(f32[2,256]{1,0:T(2,128)S(1)} %copy-done.13, f32[1024,128]{1,0:T(8,128)S(1)} %bitcast.7, f32[256,256]{1,0:T(8,128)S(1)} %copy-done.6, f32[256,256]{1,0:T(8,128)S(1)} %copy-done.5, bf16[512,256]{1,0:T(8,128)(2,1)S(1)} %copy-done.4, bf16[512,256]{1,0:T(8,128)(2,1)S(1)} %copy-done.3, ...), custom_call_target="tpu_custom_call" | custom-call | tf_op jit(solution)/shard_map/pallas_call | solution.py:310
  45.2 0.0 copy-start
  45.2 0.0 copy-start.1
  45.2 0.0 copy-start.2
  45.2 0.0 copy-start.11
  45.2 0.0 copy-start.12
  45.2 25.9 %all_to_all.11 = f32[256,4,128]{2,1,0:T(4,128)S(1)} all-to-all(f32[256,4,128]{2,1,0:T(4,128)S(1)} %bitcast.8), channel_id=1, replica_groups=mesh['grp'=8,'pen'=32] {'grp','pen'}, dimensions={0} | all-to-all | bytes 1048576 | tf_op jit(solution)/shard_map/all_to_all | solution.py:321
  71.1 0.0 copy-done
  71.1 0.0 copy-done.1
  71.1 0.0 copy-done.2
  71.1 0.0 copy-done.11
  71.1 0.0 copy-done.12
  71.1 3.9 %shard_map.169 = (f32[3,4096]{1,0:T(4,128)}, f32[1,1]{1,0:T(1,128)}) custom-call(s32[2,4096]{1,0:T(2,128)S(1)} %copy-done.11, s32[1,4096]{1,0:T(1,128)S(1)} %bitcast.12, f32[3,4096]{1,0:T(4,128)S(1)} %copy-done.2, f32[1,4096]{1,0:T(1,128)S(1)} %get-tuple-element.6.live_ref, f32[1024,128]{1,0:T(8,128)S(1)} %bitcast.9, bf16[256,256]{1,0:T(8,128)(2,1)S(1)} %copy-done.1, ...), custom_call_target="tpu_custom_call" | custom-call | tf_op jit(solution)/shard_map/pallas_call | solution.py:310
Async XLA Ops:
  0.6 39.8 %copy-start.7 = (bf16[256,320]{1,0:T(8,128)(2,1)S(1)}, bf16[256,320]{1,0:T(8,128)(2,1)}, u32[]{:S(2)}) copy-start(bf16[256,320]{1,0:T(8,128)(2,1)} %constant.30.clone.xl_ref) | copy-start | bytes 491524
  0.6 39.8 %copy-start.8 = (bf16[256,320]{1,0:T(8,128)(2,1)S(1)}, bf16[256,320]{1,0:T(8,128)(2,1)}, u32[]{:S(2)}) copy-start(bf16[256,320]{1,0:T(8,128)(2,1)} %constant.29.clone.xh_ref) | copy-start | bytes 491524
  0.7 39.8 %copy-start.13 = (f32[2,256]{1,0:T(2,128)S(1)}, f32[2,256]{1,0:T(2,128)}, u32[]{:S(2)}) copy-start(f32[2,256]{1,0:T(2,128)} %constant.24.clone.lone_ref) | copy-start | bytes 6148
  5.0 35.4 %copy-start.3 = (bf16[512,256]{1,0:T(8,128)(2,1)S(1)}, bf16[512,256]{1,0:T(8,128)(2,1)}, u32[]{:S(2)}) copy-start(bf16[512,256]{1,0:T(8,128)(2,1)} %constant.28.clone.yl_ref) | copy-start | bytes 786436
  5.0 35.4 %copy-start.4 = (bf16[512,256]{1,0:T(8,128)(2,1)S(1)}, bf16[512,256]{1,0:T(8,128)(2,1)}, u32[]{:S(2)}) copy-start(bf16[512,256]{1,0:T(8,128)(2,1)} %constant.27.clone.yh_ref) | copy-start | bytes 786436
  5.0 35.4 %copy-start.5 = (f32[256,256]{1,0:T(8,128)S(1)}, f32[256,256]{1,0:T(8,128)}, u32[]{:S(2)}) copy-start(f32[256,256]{1,0:T(8,128)} %constant.26.clone.square_ref) | copy-start | bytes 786436
  5.1 35.4 %copy-start.6 = (f32[256,256]{1,0:T(8,128)S(1)}, f32[256,256]{1,0:T(8,128)}, u32[]{:S(2)}) copy-start(f32[256,256]{1,0:T(8,128)} %constant.25.clone.factor_ref) | copy-start | bytes 786436
  40.5 0.9 %copy-start.9 = (bf16[320,256]{1,0:T(8,128)(2,1)S(1)}, bf16[320,256]{1,0:T(8,128)(2,1)}, u32[]{:S(2)}) copy-start(bf16[320,256]{1,0:T(8,128)(2,1)} %constant.32.clone.xtl_ref) | copy-start | bytes 491524
  41.4 0.9 %copy-start.10 = (bf16[320,256]{1,0:T(8,128)(2,1)S(1)}, bf16[320,256]{1,0:T(8,128)(2,1)}, u32[]{:S(2)}) copy-start(bf16[320,256]{1,0:T(8,128)(2,1)} %constant.31.clone.xth_ref) | copy-start | bytes 491524
  45.2 25.9 %copy-start = (bf16[256,256]{1,0:T(8,128)(2,1)S(1)}, bf16[256,256]{1,0:T(8,128)(2,1)}, u32[]{:S(2)}) copy-start(bf16[256,256]{1,0:T(8,128)(2,1)} %constant.23.clone.low_hbm.low_ref) | copy-start | bytes 393220
  45.2 25.9 %copy-start.1 = (bf16[256,256]{1,0:T(8,128)(2,1)S(1)}, bf16[256,256]{1,0:T(8,128)(2,1)}, u32[]{:S(2)}) copy-start(bf16[256,256]{1,0:T(8,128)(2,1)} %constant.22.clone.high_hbm.high_ref) | copy-start | bytes 393220
  45.2 25.9 %copy-start.2 = (f32[3,4096]{1,0:T(4,128)S(1)}, f32[3,4096]{1,0:T(4,128)}, u32[]{:S(2)}) copy-start(f32[3,4096]{1,0:T(4,128)} %frac_ref.1) | copy-start | bytes 147460
  45.2 25.9 %copy-start.11 = (s32[2,4096]{1,0:T(2,128)S(1)}, s32[2,4096]{1,0:T(2,128)}, u32[]{:S(2)}) copy-start(s32[2,4096]{1,0:T(2,128)} %offsets_ref.1) | copy-start | bytes 98308
  45.2 25.9 %copy-start.12 = (s32[4096]{0:T(1024)S(1)}, s32[4096]{0:T(1024)}, u32[]{:S(2)}) copy-start(s32[4096]{0:T(1024)} %param.17) | copy-start | bytes 49156

commit v3 on v2

--- a/solution.py
+++ b/solution.py
@@ -25,6 +25,7 @@
 ROWS = 16 * (2 * TILES_X + 6)
 ROW_X = 40
 SPARE = 16
+GROUP = 4
 F32 = jnp.float32
 BF16 = jnp.bfloat16
 
@@ -60,12 +61,9 @@
     lone = np.stack([factor, square])
     return dict(
         full=halves(full),
-        y=halves(table_y),
-        x=halves(table_x),
-        xt=halves(table_x.T),
-        factor=plane_factor.astype(np.float32),
-        square=plane_square.astype(np.float32),
-        lone=lone.astype(np.float32),
+        wide=np.concatenate([*halves(table_y), *halves(table_x.T)]),
+        x=np.concatenate(halves(table_x)),
+        plane=np.concatenate([plane_factor, plane_square, lone]).astype(np.float32),
     )
 
 
@@ -83,9 +81,9 @@
 
 
 def dot3(left, right, dims=((1,), (0,))):
-    return (
-        dot(left[0], right[0], dims) + dot(left[1], right[0], dims) + dot(left[0], right[1], dims)
-    )
+    size = left[0].shape[0]
+    both = dot(jnp.concatenate(left, axis=0), right[0], dims)
+    return both[:size] + both[size:] + dot(left[0], right[1], dims)
 
 
 def spline_rows(fracs):
@@ -127,18 +125,29 @@
     return value
 
 
-def column_parts(column, offsets_ref, cell_z_ref, frac_ref):
-    lanes = pl.ds(pl.multiple_of(column * 256, 256), 256)
-    values, slopes = spline_rows(frac_ref[:, lanes])
+def column_lanes(column):
+    return pl.ds(pl.multiple_of(column * 256, 256), 256)
+
+
+def group_splines(group, frac_ref):
+    fracs = [frac_ref[:, column_lanes(GROUP * group + c)] for c in range(GROUP)]
+    return spline_rows(jnp.concatenate(fracs, axis=0))
+
+
+def column_parts(group, c, splines, offsets_ref, cell_z_ref):
+    column = GROUP * group + c
+    lanes = column_lanes(column)
+    rows, grades = [
+        [[value[3 * c + d : 3 * c + d + 1, :] for value in values] for d in range(3)]
+        for values in splines
+    ]
     tile = iota((1, 256), 1) // 64
-    rows = [[value[d : d + 1, :] for value in values] for d in range(3)]
-    grades = [[slope[d : d + 1, :] for slope in slopes] for d in range(3)]
     from_x = iota((8, 256), 0) - offsets_ref[0:1, lanes]
     from_y = iota((16, 256), 0) - (offsets_ref[1:2, lanes] + 2 * tile)
     cell_z = cell_z_ref[:, lanes]
     from_z = (iota((16, 256), 0) - cell_z) & 15
     owner_z = (((cell_z + from_z) & (K - 1)) >> 4).astype(F32).astype(BF16)
-    return lanes, rows, grades, from_x, from_y, from_z, owner_z
+    return column, lanes, rows, grades, from_x, from_y, from_z, owner_z
 
 
 def along_z(from_z, owner_z, rows):
@@ -167,23 +176,25 @@
     for copy in copies[:5]:
         copy.wait()
 
-    @pl.loop(0, TILES_X, unroll=4)
-    def _(column):
-        lanes, rows, grades, from_x, from_y, from_z, owner_z = column_parts(
-            column, offsets_ref, cell_z_ref, frac_ref
-        )
-        lane = iota((1, 256), 1)
-        counts = jnp.full((1, 256), counts_ref[4 * column], jnp.int32)
-        for b in range(1, 4):
-            counts = jnp.where(lane // 64 == b, counts_ref[4 * column + b], counts)
-        live_q = jnp.where(lane % 64 < counts, charges_ref[:, lanes], 0.0)
-        live_ref[:, lanes] = live_q
-        weight_x = pick(from_x, rows[0]) * live_q
-        weight_y = pick(from_y, rows[1])
-        pair = jnp.concatenate([weight_x[i : i + 1, :] * weight_y for i in range(8)], axis=0)
-        weight_z = along_z(from_z, owner_z, rows[2])
-        place = pl.ds(pl.multiple_of(column * 32, 32), 128)
-        mesh_ref[place, :] += dot3(split(pair), weight_z, ((1,), (1,)))
+    @pl.loop(0, TILES_X // GROUP)
+    def _(group):
+        splines = group_splines(group, frac_ref)
+        for c in range(GROUP):
+            column, lanes, rows, grades, from_x, from_y, from_z, owner_z = column_parts(
+                group, c, splines, offsets_ref, cell_z_ref
+            )
+            lane = iota((1, 256), 1)
+            counts = jnp.full((1, 256), counts_ref[4 * column], jnp.int32)
+            for b in range(1, 4):
+                counts = jnp.where(lane // 64 == b, counts_ref[4 * column + b], counts)
+            live_q = jnp.where(lane % 64 < counts, charges_ref[:, lanes], 0.0)
+            live_ref[:, lanes] = live_q
+            weight_x = pick(from_x, rows[0]) * live_q
+            weight_y = pick(from_y, rows[1])
+            pair = jnp.concatenate([weight_x[i : i + 1, :] * weight_y for i in range(8)], axis=0)
+            weight_z = along_z(from_z, owner_z, rows[2])
+            place = pl.ds(pl.multiple_of(column * 32, 32), 128)
+            mesh_ref[place, :] += dot3(split(pair), weight_z, ((1,), (1,)))
 
     for x in range(PAD_X):
         packed_ref[PAD_Y * x : PAD_Y * (x + 1), :] = mesh_ref[16 * x : 16 * x + PAD_Y, :]
@@ -196,8 +207,7 @@
 
 
 def plane_kernel(
-    lone_ref, in_ref, factor_ref, square_ref, yh_ref, yl_ref, xh_ref, xl_ref, xth_ref, xtl_ref,
-    out_ref, turned_ref, wide_ref,
+    in_ref, plane_ref, table_ref, x_ref, out_ref, turned_ref, wide_ref
 ):
     for j in range(4):
         turned = in_ref[pl.ds(j, 256, stride=4), :].T
@@ -217,21 +227,22 @@
                         piece = pltpu.roll(piece, shift, 1)
                     block = jnp.where(section == s, piece, block)
             wide_ref[ROW_X * g : ROW_X * (g + 1), 128 * quad : 128 * quad + 128] = block
-    table_y = (yh_ref[...], yl_ref[...])
+    table_y = (table_ref[:CHUNK, :], table_ref[CHUNK : 2 * CHUNK, :])
+    table_xt = (table_ref[2 * CHUNK : 2 * CHUNK + 320, :], table_ref[2 * CHUNK + 320 :, :])
     half = dot3(split(wide_ref[...]), table_y)
-    spectrum = dot3((xh_ref[...], xl_ref[...]), split(half))
+    spectrum = dot3((x_ref[:K, :], x_ref[K:, :]), split(half))
     mode = lax.axis_index("grp") * N_PEN + lax.axis_index("pen")
-    lone = jnp.where(iota((2, 256), 1) == mode, lone_ref[...], 0.0)
+    lone = jnp.where(iota((2, 256), 1) == mode, plane_ref[2 * K :, :], 0.0)
     lone = jnp.sum(lone, axis=1, keepdims=True)
-    square = square_ref[...] + lone[1:2, :]
+    square = plane_ref[K : 2 * K, :] + lone[1:2, :]
     nonzero = square > 0
     kernel = jnp.where(
-        nonzero, factor_ref[...] * lone[0:1, :] / jnp.where(nonzero, square, 1.0), 0.0
+        nonzero, plane_ref[:K, :] * lone[0:1, :] / jnp.where(nonzero, square, 1.0), 0.0
     )
     scaled = kernel * spectrum
     energy = jnp.sum(jnp.sum(scaled * spectrum, axis=0, keepdims=True), axis=1, keepdims=True)
     energy = energy * (0.5 / ATOMS)
-    back = dot3((xth_ref[...], xtl_ref[...]), split(scaled))
+    back = dot3(table_xt, split(scaled))
     wide_ref[...] = dot3(split(back), table_y, ((1,), (1,)))
     for y in range(PAD_Y):
         for h in range(2):
@@ -278,31 +289,33 @@
     mesh_high_ref[16 * PAD_X :, :] = jnp.zeros((ROWS - 16 * PAD_X, 256), BF16)
     mesh_low_ref[16 * PAD_X :, :] = jnp.zeros((ROWS - 16 * PAD_X, 256), BF16)
 
-    @pl.loop(0, TILES_X, unroll=4)
-    def _(column):
-        lanes, rows, grades, from_x, from_y, from_z, owner_z = column_parts(
-            column, offsets_ref, cell_z_ref, frac_ref
-        )
-        live_q = live_ref[:, lanes]
-        weight_x = pick(from_x, rows[0])
-        grade_x = pick(from_x, grades[0])
-        weight_y = pick(from_y, rows[1])
-        grade_y = pick(from_y, grades[1])
-        place = pl.ds(pl.multiple_of(column * 32, 32), 128)
-        footing = (mesh_high_ref[place, :], mesh_low_ref[place, :])
-        main = dot3(footing, along_z(from_z, owner_z, rows[2]))
-        tilt = dot3(footing, along_z(from_z, owner_z, grades[2]))
-        sum_x = 0.0
-        sum_y = 0.0
-        sum_z = 0.0
-        for i in range(8):
-            band = main[16 * i : 16 * i + 16, :]
-            sum_x = sum_x + grade_x[i : i + 1, :] * band
-            sum_y = sum_y + weight_x[i : i + 1, :] * band
-            sum_z = sum_z + weight_x[i : i + 1, :] * tilt[16 * i : 16 * i + 16, :]
-        forces_ref[0:1, lanes] = -live_q * jnp.sum(weight_y * sum_x, axis=0, keepdims=True)
-        forces_ref[1:2, lanes] = -live_q * jnp.sum(grade_y * sum_y, axis=0, keepdims=True)
-        forces_ref[2:3, lanes] = -live_q * jnp.sum(weight_y * sum_z, axis=0, keepdims=True)
+    @pl.loop(0, TILES_X // GROUP)
+    def _(group):
+        splines = group_splines(group, frac_ref)
+        for c in range(GROUP):
+            column, lanes, rows, grades, from_x, from_y, from_z, owner_z = column_parts(
+                group, c, splines, offsets_ref, cell_z_ref
+            )
+            live_q = live_ref[:, lanes]
+            weight_x = pick(from_x, rows[0])
+            grade_x = pick(from_x, grades[0])
+            weight_y = pick(from_y, rows[1])
+            grade_y = pick(from_y, grades[1])
+            place = pl.ds(pl.multiple_of(column * 32, 32), 128)
+            footing = (mesh_high_ref[place, :], mesh_low_ref[place, :])
+            main = dot3(footing, along_z(from_z, owner_z, rows[2]))
+            tilt = dot3(footing, along_z(from_z, owner_z, grades[2]))
+            sum_x = 0.0
+            sum_y = 0.0
+            sum_z = 0.0
+            for i in range(8):
+                band = main[16 * i : 16 * i + 16, :]
+                sum_x = sum_x + grade_x[i : i + 1, :] * band
+                sum_y = sum_y + weight_x[i : i + 1, :] * band
+                sum_z = sum_z + weight_x[i : i + 1, :] * tilt[16 * i : 16 * i + 16, :]
+            forces_ref[0:1, lanes] = -live_q * jnp.sum(weight_y * sum_x, axis=0, keepdims=True)
+            forces_ref[1:2, lanes] = -live_q * jnp.sum(grade_y * sum_y, axis=0, keepdims=True)
+            forces_ref[2:3, lanes] = -live_q * jnp.sum(weight_y * sum_z, axis=0, keepdims=True)
 
 
 def call(kernel, out_shape, scratch, *args, memory=pltpu.VMEM):
@@ -313,7 +326,8 @@
         in_specs=[pl.BlockSpec(memory_space=memory)] * len(args),
         out_specs=jax.tree.map(lambda _: vmem, out_shape),
         scratch_shapes=scratch,
-        compiler_params=pltpu.CompilerParams(vmem_limit_bytes=16 * 1024 * 1024),
+        compiler_params=pltpu.CompilerParams(vmem_limit_bytes=8 * 1024 * 1024),
+        cost_estimate=pl.CostEstimate(flops=3 * 10**9, bytes_accessed=10**7, transcendentals=0),
     )(*args)
 
 
@@ -342,14 +356,12 @@
         memory=pltpu.HBM,
     )
     plane = exchange(outgoing)
-    planes = [TABLES["factor"], TABLES["square"], *TABLES["y"], *TABLES["x"], *TABLES["xt"]]
     returning = call(
         plane_kernel,
         block,
         [pltpu.VMEM((2, CHUNK + SPARE, 128), F32), pltpu.VMEM((N_GRP * ROW_X, CHUNK), F32)],
-        jnp.asarray(TABLES["lone"]),
         plane,
-        *[jnp.asarray(value) for value in planes],
+        *[jnp.asarray(TABLES[name]) for name in ("plane", "wide", "x")],
     )
     home = exchange(returning)
     forces, energy = call(

time: 75.2 us -> 72.5 us (0.964)
  local copies, waits for them, and re-layouts: 1.91 us -> 0.05 us
  Pallas kernels: 11.1 us -> 10.3 us
    unnamed x28 -> x16, local copies, waits for them, and re-layouts: 1.91 us -> 0.05 us
    pallas_call x3, Pallas kernels: 11.1 us -> 10.3 us  [call(): pl.pallas_call(kernel, out_shape=out_shape, in_specs=[pl.BlockSpec(memory...]
where the time goes in v3:
time: 72.5 us; the launch traced here: 72.3 us
  blocking collectives  61.2 us (84%)
  Pallas kernels  10.3 us (14%)
  between operations  0.73 us (1%)
    all_to_all x2, blocking collectives, exchange(): lax.all_to_all(block.reshape(256, 4, 128), AXES, 0, 0, tiled=True)  61.2 us
    pallas_call x3, Pallas kernels, call(): pl.pallas_call(kernel, out_shape=out_shape, in_specs=[pl.BlockSpec(memory...  10.3 us

profile of v3, /device:TPU:1, one launch (start us, length us, event | category | flops | bytes accessed | tf_op | source)
XLA Modules:
  0.0 72.3 jit_solution(16347437797861516038)
XLA Ops:
  0.6 0.0 copy-start.4
  0.6 0.0 copy-start.5
  0.7 3.7 %shard_map.113 = (f32[1024,128]{1,0:T(8,128)S(1)}, f32[1,4096]{1,0:T(1,128)S(1)}) custom-call(s32[64]{0:T(128)} %counts_hbm.1, s32[2,4096]{1,0:T(2,128)} %offsets_ref.1, s32[1,4096]{1,0:T(1,128)} %bitcast.11, f32[3,4096]{1,0:T(4,128)} %frac_ref.1, f32[1,4096]{1,0:T(1,128)} %bitcast.13, bf16[256,256]{1,0:T(8,128)(2,1)} %constant.10.clone.high_hbm.high_ref, ...), custom_call_target="tpu_custom_call" | custom-call | flops 3000000000 | bytes 10000000 | tf_op jit(solution)/shard_map/pallas_call | solution.py:323
  4.4 0.0 copy-start.3
  4.4 35.3 %all_to_all.10 = f32[256,4,128]{2,1,0:T(4,128)S(1)} all-to-all(f32[256,4,128]{2,1,0:T(4,128)S(1)} %bitcast.10), channel_id=1, replica_groups=mesh['grp'=8,'pen'=32] {'grp','pen'}, dimensions={0} | all-to-all | bytes 1048576 | tf_op jit(solution)/shard_map/all_to_all | solution.py:335
  39.7 0.0 copy-done.4
  39.7 0.0 copy-done.5
  39.7 0.0 copy-done.3
  39.7 2.8 %shard_map.114 = f32[1024,128]{1,0:T(8,128)S(1)} custom-call(f32[1024,128]{1,0:T(8,128)S(1)} %bitcast.8, f32[514,256]{1,0:T(8,128)S(1)} %copy-done.4, bf16[1664,256]{1,0:T(8,128)(2,1)S(1)} %copy-done.3, bf16[512,320]{1,0:T(8,128)(2,1)S(1)} %copy-done.5), custom_call_target="tpu_custom_call" | custom-call | flops 3000000000 | bytes 10000000 | tf_op jit(solution)/shard_map/pallas_call | solution.py:323
  42.5 0.0 copy-start
  42.5 0.0 copy-start.1
  42.5 0.0 copy-start.2
  42.5 0.0 copy-start.6
  42.5 0.0 copy-start.7
  42.6 25.9 %all_to_all.11 = f32[256,4,128]{2,1,0:T(4,128)S(1)} all-to-all(f32[256,4,128]{2,1,0:T(4,128)S(1)} %bitcast.9), channel_id=1, replica_groups=mesh['grp'=8,'pen'=32] {'grp','pen'}, dimensions={0} | all-to-all | bytes 1048576 | tf_op jit(solution)/shard_map/all_to_all | solution.py:335
  68.4 0.0 copy-done
  68.4 0.0 copy-done.1
  68.4 0.0 copy-done.2
  68.4 0.0 copy-done.6
  68.5 0.0 copy-done.7
  68.5 3.8 %shard_map.115 = (f32[3,4096]{1,0:T(4,128)}, f32[1,1]{1,0:T(1,128)}) custom-call(s32[2,4096]{1,0:T(2,128)S(1)} %copy-done.1, s32[1,4096]{1,0:T(1,128)S(1)} %bitcast.12, f32[3,4096]{1,0:T(4,128)S(1)} %copy-done, f32[1,4096]{1,0:T(1,128)S(1)} %get-tuple-element.6.live_ref, f32[1024,128]{1,0:T(8,128)S(1)} %bitcast.7, bf16[256,256]{1,0:T(8,128)(2,1)S(1)} %copy-done.7, ...), custom_call_target="tpu_custom_call" | custom-call | flops 3000000000 | bytes 10000000 | tf_op jit(solution)/shard_map/pallas_call | solution.py:323
Async XLA Ops:
  0.6 39.1 %copy-start.4 = (f32[514,256]{1,0:T(8,128)S(1)}, f32[514,256]{1,0:T(8,128)}, u32[]{:S(2)}) copy-start(f32[514,256]{1,0:T(8,128)} %constant.12.clone.plane_ref) | copy-start | bytes 1579012
  0.6 39.1 %copy-start.5 = (bf16[512,320]{1,0:T(8,128)(2,1)S(1)}, bf16[512,320]{1,0:T(8,128)(2,1)}, u32[]{:S(2)}) copy-start(bf16[512,320]{1,0:T(8,128)(2,1)} %constant.14.clone.x_ref) | copy-start | bytes 983044
  4.4 35.4 %copy-start.3 = (bf16[1664,256]{1,0:T(8,128)(2,1)S(1)}, bf16[1664,256]{1,0:T(8,128)(2,1)}, u32[]{:S(2)}) copy-start(bf16[1664,256]{1,0:T(8,128)(2,1)} %constant.13.clone.table_ref) | copy-start | bytes 2555908
  42.5 25.9 %copy-start = (f32[3,4096]{1,0:T(4,128)S(1)}, f32[3,4096]{1,0:T(4,128)}, u32[]{:S(2)}) copy-start(f32[3,4096]{1,0:T(4,128)} %frac_ref.1) | copy-start | bytes 147460
  42.5 25.9 %copy-start.1 = (s32[2,4096]{1,0:T(2,128)S(1)}, s32[2,4096]{1,0:T(2,128)}, u32[]{:S(2)}) copy-start(s32[2,4096]{1,0:T(2,128)} %offsets_ref.1) | copy-start | bytes 98308
  42.5 25.9 %copy-start.2 = (s32[4096]{0:T(1024)S(1)}, s32[4096]{0:T(1024)}, u32[]{:S(2)}) copy-start(s32[4096]{0:T(1024)} %param.11) | copy-start | bytes 49156
  42.5 25.9 %copy-start.6 = (bf16[256,256]{1,0:T(8,128)(2,1)S(1)}, bf16[256,256]{1,0:T(8,128)(2,1)}, u32[]{:S(2)}) copy-start(bf16[256,256]{1,0:T(8,128)(2,1)} %constant.11.clone.low_hbm.low_ref) | copy-start | bytes 393220
  42.5 25.9 %copy-start.7 = (bf16[256,256]{1,0:T(8,128)(2,1)S(1)}, bf16[256,256]{1,0:T(8,128)(2,1)}, u32[]{:S(2)}) copy-start(bf16[256,256]{1,0:T(8,128)(2,1)} %constant.10.clone.high_hbm.high_ref) | copy-start | bytes 393220

commit v4 on v3

--- a/solution.py
+++ b/solution.py
@@ -25,7 +25,7 @@
 ROWS = 16 * (2 * TILES_X + 6)
 ROW_X = 40
 SPARE = 16
-GROUP = 4
+GROUP = 16
 F32 = jnp.float32
 BF16 = jnp.bfloat16
 

time: 72.5 us -> 71.6 us (0.988)
  Pallas kernels: 10.3 us -> 9.42 us
    pallas_call x3, Pallas kernels: 10.3 us -> 9.42 us  [call(): pl.pallas_call(kernel, out_shape=out_shape, in_specs=[pl.BlockSpec(memory...]
where the time goes in v4:
time: 71.6 us; the launch traced here: 71.4 us
  blocking collectives  61.2 us (85%)
  Pallas kernels  9.42 us (13%)
  between operations  0.73 us (1%)
    all_to_all x2, blocking collectives, exchange(): lax.all_to_all(block.reshape(256, 4, 128), AXES, 0, 0, tiled=True)  61.2 us
    pallas_call x3, Pallas kernels, call(): pl.pallas_call(kernel, out_shape=out_shape, in_specs=[pl.BlockSpec(memory...  9.42 us

profile of v4, /device:TPU:1, one launch (start us, length us, event | category | flops | bytes accessed | tf_op | source)
XLA Modules:
  0.0 71.4 jit_solution(4502251517557081805)
XLA Ops:
  0.6 0.0 copy-start.4
  0.6 0.0 copy-start.5
  0.7 3.3 %shard_map.113 = (f32[1024,128]{1,0:T(8,128)S(1)}, f32[1,4096]{1,0:T(1,128)S(1)}) custom-call(s32[64]{0:T(128)} %counts_hbm.1, s32[2,4096]{1,0:T(2,128)} %offsets_ref.1, s32[1,4096]{1,0:T(1,128)} %bitcast.11, f32[3,4096]{1,0:T(4,128)} %frac_ref.1, f32[1,4096]{1,0:T(1,128)} %bitcast.13, bf16[256,256]{1,0:T(8,128)(2,1)} %constant.10.clone.high_hbm.high_ref, ...), custom_call_target="tpu_custom_call" | custom-call | flops 3000000000 | bytes 10000000 | tf_op jit(solution)/shard_map/pallas_call | solution.py:323
  4.0 0.0 copy-start.3
  4.0 35.3 %all_to_all.10 = f32[256,4,128]{2,1,0:T(4,128)S(1)} all-to-all(f32[256,4,128]{2,1,0:T(4,128)S(1)} %bitcast.10), channel_id=1, replica_groups=mesh['grp'=8,'pen'=32] {'grp','pen'}, dimensions={0} | all-to-all | bytes 1048576 | tf_op jit(solution)/shard_map/all_to_all | solution.py:335
  39.4 0.0 copy-done.4
  39.4 0.0 copy-done.5
  39.4 0.0 copy-done.3
  39.4 2.8 %shard_map.114 = f32[1024,128]{1,0:T(8,128)S(1)} custom-call(f32[1024,128]{1,0:T(8,128)S(1)} %bitcast.8, f32[514,256]{1,0:T(8,128)S(1)} %copy-done.4, bf16[1664,256]{1,0:T(8,128)(2,1)S(1)} %copy-done.3, bf16[512,320]{1,0:T(8,128)(2,1)S(1)} %copy-done.5), custom_call_target="tpu_custom_call" | custom-call | flops 3000000000 | bytes 10000000 | tf_op jit(solution)/shard_map/pallas_call | solution.py:323
  42.1 0.0 copy-start
  42.1 0.0 copy-start.1
  42.2 0.0 copy-start.2
  42.2 0.0 copy-start.6
  42.2 0.0 copy-start.7
  42.2 25.9 %all_to_all.11 = f32[256,4,128]{2,1,0:T(4,128)S(1)} all-to-all(f32[256,4,128]{2,1,0:T(4,128)S(1)} %bitcast.9), channel_id=1, replica_groups=mesh['grp'=8,'pen'=32] {'grp','pen'}, dimensions={0} | all-to-all | bytes 1048576 | tf_op jit(solution)/shard_map/all_to_all | solution.py:335
  68.1 0.0 copy-done
  68.1 0.0 copy-done.1
  68.1 0.0 copy-done.2
  68.1 0.0 copy-done.6
  68.1 0.0 copy-done.7
  68.1 3.3 %shard_map.115 = (f32[3,4096]{1,0:T(4,128)}, f32[1,1]{1,0:T(1,128)}) custom-call(s32[2,4096]{1,0:T(2,128)S(1)} %copy-done.1, s32[1,4096]{1,0:T(1,128)S(1)} %bitcast.12, f32[3,4096]{1,0:T(4,128)S(1)} %copy-done, f32[1,4096]{1,0:T(1,128)S(1)} %get-tuple-element.6.live_ref, f32[1024,128]{1,0:T(8,128)S(1)} %bitcast.7, bf16[256,256]{1,0:T(8,128)(2,1)S(1)} %copy-done.7, ...), custom_call_target="tpu_custom_call" | custom-call | flops 3000000000 | bytes 10000000 | tf_op jit(solution)/shard_map/pallas_call | solution.py:323
Async XLA Ops:
  0.6 38.7 %copy-start.4 = (f32[514,256]{1,0:T(8,128)S(1)}, f32[514,256]{1,0:T(8,128)}, u32[]{:S(2)}) copy-start(f32[514,256]{1,0:T(8,128)} %constant.12.clone.plane_ref) | copy-start | bytes 1579012
  0.6 38.7 %copy-start.5 = (bf16[512,320]{1,0:T(8,128)(2,1)S(1)}, bf16[512,320]{1,0:T(8,128)(2,1)}, u32[]{:S(2)}) copy-start(bf16[512,320]{1,0:T(8,128)(2,1)} %constant.14.clone.x_ref) | copy-start | bytes 983044
  4.0 35.4 %copy-start.3 = (bf16[1664,256]{1,0:T(8,128)(2,1)S(1)}, bf16[1664,256]{1,0:T(8,128)(2,1)}, u32[]{:S(2)}) copy-start(bf16[1664,256]{1,0:T(8,128)(2,1)} %constant.13.clone.table_ref) | copy-start | bytes 2555908
  42.1 25.9 %copy-start = (f32[3,4096]{1,0:T(4,128)S(1)}, f32[3,4096]{1,0:T(4,128)}, u32[]{:S(2)}) copy-start(f32[3,4096]{1,0:T(4,128)} %frac_ref.1) | copy-start | bytes 147460
  42.1 25.9 %copy-start.1 = (s32[2,4096]{1,0:T(2,128)S(1)}, s32[2,4096]{1,0:T(2,128)}, u32[]{:S(2)}) copy-start(s32[2,4096]{1,0:T(2,128)} %offsets_ref.1) | copy-start | bytes 98308
  42.2 25.9 %copy-start.2 = (s32[4096]{0:T(1024)S(1)}, s32[4096]{0:T(1024)}, u32[]{:S(2)}) copy-start(s32[4096]{0:T(1024)} %param.11) | copy-start | bytes 49156
  42.2 25.9 %copy-start.6 = (bf16[256,256]{1,0:T(8,128)(2,1)S(1)}, bf16[256,256]{1,0:T(8,128)(2,1)}, u32[]{:S(2)}) copy-start(bf16[256,256]{1,0:T(8,128)(2,1)} %constant.11.clone.low_hbm.low_ref) | copy-start | bytes 393220
  42.2 25.9 %copy-start.7 = (bf16[256,256]{1,0:T(8,128)(2,1)S(1)}, bf16[256,256]{1,0:T(8,128)(2,1)}, u32[]{:S(2)}) copy-start(bf16[256,256]{1,0:T(8,128)(2,1)} %constant.10.clone.high_hbm.high_ref) | copy-start | bytes 393220

commit v5 on v4

--- a/solution.py
+++ b/solution.py
@@ -22,7 +22,7 @@
 PAD_Y = BLOCK_Y + 5
 USED = PAD_X * PAD_Y
 CHUNK = 512
-ROWS = 16 * (2 * TILES_X + 6)
+ROWS = 16 * PAD_X
 ROW_X = 40
 SPARE = 16
 GROUP = 16
@@ -44,12 +44,7 @@
 def make_tables():
     index = np.arange(K)
     full = cas(index, index)
-    spread_y = (BLOCK_Y * np.arange(N_PEN)[None, :] + np.arange(16)[:, None]).reshape(-1)
-    valid_y = np.repeat(np.arange(16) < PAD_Y, N_PEN)
-    table_y = cas(spread_y, index) * valid_y[:, None]
-    spread_x = (BLOCK_X * np.arange(N_GRP)[:, None] + np.arange(ROW_X)[None, :]).reshape(-1)
-    valid_x = np.tile(np.arange(ROW_X) < PAD_X, N_GRP)
-    table_x = cas(index, spread_x) * valid_x[None, :]
+    order_y = (BLOCK_Y * np.arange(N_PEN)[None, :] + np.arange(BLOCK_Y)[:, None]).reshape(-1)
     frequency = np.where(2 * index < K, index, index - K) / K
     square = frequency * frequency
     coeffs = np.array([1.0, 26.0, 66.0, 26.0, 1.0]) / 120.0
@@ -60,9 +55,8 @@
     plane_square = square[:, None] + square[None, :]
     lone = np.stack([factor, square])
     return dict(
-        full=halves(full),
-        wide=np.concatenate([*halves(table_y), *halves(table_x.T)]),
-        x=np.concatenate(halves(table_x)),
+        full=np.concatenate(halves(full)),
+        order=np.concatenate(halves(full[order_y])),
         plane=np.concatenate([plane_factor, plane_square, lone]).astype(np.float32),
     )
 
@@ -160,12 +154,12 @@
 
 
 def spread_kernel(
-    counts_hbm, offsets_hbm, cell_z_hbm, frac_hbm, charges_hbm, high_hbm, low_hbm, out_ref, live_ref,
-    mesh_ref, packed_ref, counts_ref, offsets_ref, cell_z_ref, frac_ref, charges_ref, high_ref,
-    low_ref, sems,
+    counts_hbm, offsets_hbm, cell_z_hbm, frac_hbm, charges_hbm, table_hbm, out_ref, live_ref,
+    mesh_ref, packed_ref, counts_ref, offsets_ref, cell_z_ref, frac_ref, charges_ref, table_ref,
+    sems,
 ):
-    sources = [counts_hbm, offsets_hbm, cell_z_hbm, frac_hbm, charges_hbm, high_hbm, low_hbm]
-    targets = [counts_ref, offsets_ref, cell_z_ref, frac_ref, charges_ref, high_ref, low_ref]
+    sources = [counts_hbm, offsets_hbm, cell_z_hbm, frac_hbm, charges_hbm, table_hbm]
+    targets = [counts_ref, offsets_ref, cell_z_ref, frac_ref, charges_ref, table_ref]
     copies = [
         pltpu.make_async_copy(source, target, sems.at[i])
         for i, (source, target) in enumerate(zip(sources, targets))
@@ -191,9 +185,9 @@
             live_ref[:, lanes] = live_q
             weight_x = pick(from_x, rows[0]) * live_q
             weight_y = pick(from_y, rows[1])
-            pair = jnp.concatenate([weight_x[i : i + 1, :] * weight_y for i in range(8)], axis=0)
+            pair = jnp.concatenate([weight_x[i : i + 1, :] * weight_y for i in range(7)], axis=0)
             weight_z = along_z(from_z, owner_z, rows[2])
-            place = pl.ds(pl.multiple_of(column * 32, 32), 128)
+            place = pl.ds(pl.multiple_of(column * 32, 32), 112)
             mesh_ref[place, :] += dot3(split(pair), weight_z, ((1,), (1,)))
 
     for x in range(PAD_X):
@@ -201,36 +195,58 @@
     packed_ref[USED:, :] = jnp.zeros((CHUNK - USED, 256), F32)
     for copy in copies[5:]:
         copy.wait()
-    spectrum = dot3((high_ref[...], low_ref[...]), split(packed_ref[...]), ((1,), (1,)))
+    spectrum = dot3((table_ref[:K, :], table_ref[K:, :]), split(packed_ref[...]), ((1,), (1,)))
     for j in range(4):
         out_ref[pl.ds(j, 256, stride=4), :] = spectrum[:, 128 * j : 128 * j + 128]
 
 
-def plane_kernel(
-    in_ref, plane_ref, table_ref, x_ref, out_ref, turned_ref, wide_ref
-):
+def regroup(pieces, own, section):
+    block = None
+    for s, piece in enumerate(pieces):
+        shift = (32 * (s - own)) % 128
+        if shift:
+            piece = pltpu.roll(piece, shift, 1)
+        block = piece if block is None else jnp.where(section == s, piece, block)
+    return block
+
+
+def to_next(value, place):
+    return jnp.where(place == 0, pltpu.roll(value, 97, 1), pltpu.roll(value, 1, 1))
+
+
+def to_previous(value, place):
+    return jnp.where(place == 31, pltpu.roll(value, 31, 1), pltpu.roll(value, 127, 1))
+
+
+def plane_kernel(in_ref, plane_ref, order_ref, table_ref, out_ref, turned_ref, wide_ref):
     for j in range(4):
         turned = in_ref[pl.ds(j, 256, stride=4), :].T
         for h in range(2):
             turned_ref[h, 128 * j : 128 * j + 128, :] = turned[:, 128 * h : 128 * h + 128]
     turned_ref[:, CHUNK:, :] = jnp.zeros((2, SPARE, 128), F32)
-    section = iota((ROW_X, 128), 1) // 32
-    for g in range(N_GRP):
-        for quad in range(4):
-            block = jnp.zeros((ROW_X, 128), F32)
-            for s in range(4):
-                y = 4 * quad + s
-                if y < PAD_Y:
-                    piece = turned_ref[g // 4, pl.ds(y, ROW_X, stride=PAD_Y), :]
-                    shift = (32 * (s - g % 4)) % 128
-                    if shift:
-                        piece = pltpu.roll(piece, shift, 1)
-                    block = jnp.where(section == s, piece, block)
-            wide_ref[ROW_X * g : ROW_X * (g + 1), 128 * quad : 128 * quad + 128] = block
-    table_y = (table_ref[:CHUNK, :], table_ref[CHUNK : 2 * CHUNK, :])
-    table_xt = (table_ref[2 * CHUNK : 2 * CHUNK + 320, :], table_ref[2 * CHUNK + 320 :, :])
-    half = dot3(split(wide_ref[...]), table_y)
-    spectrum = dot3((x_ref[:K, :], x_ref[K:, :]), split(half))
+    lane = iota((ROW_X, 128), 1)
+    section = lane // 32
+    place = lane % 32
+    merged = []
+    for h in range(2):
+        lines = [turned_ref[h, pl.ds(y, ROW_X, stride=PAD_Y), :] for y in range(PAD_Y)]
+        for y in range(PAD_Y - BLOCK_Y):
+            lines[y] = lines[y] + to_next(lines[y + BLOCK_Y], place)
+        merged.append(lines[:BLOCK_Y])
+    beyond = iota((8, 128), 0) < PAD_X - BLOCK_X
+    for quad in range(2):
+        blocks = [
+            regroup(merged[g // 4][4 * quad : 4 * quad + 4], g % 4, section) for g in range(N_GRP)
+        ]
+        for g in range(N_GRP):
+            halo = jnp.where(beyond, blocks[g - 1][BLOCK_X:], 0.0)
+            columns = slice(128 * quad, 128 * quad + 128)
+            wide_ref[BLOCK_X * g : BLOCK_X * g + 8, columns] = blocks[g][:8] + halo
+            wide_ref[BLOCK_X * g + 8 : BLOCK_X * (g + 1), columns] = blocks[g][8:BLOCK_X]
+    order = (order_ref[:K, :], order_ref[K:, :])
+    table = (table_ref[:K, :], table_ref[K:, :])
+    half = dot3(split(wide_ref[...]), order)
+    spectrum = dot3(table, split(half))
     mode = lax.axis_index("grp") * N_PEN + lax.axis_index("pen")
     lone = jnp.where(iota((2, 256), 1) == mode, plane_ref[2 * K :, :], 0.0)
     lone = jnp.sum(lone, axis=1, keepdims=True)
@@ -242,37 +258,46 @@
     scaled = kernel * spectrum
     energy = jnp.sum(jnp.sum(scaled * spectrum, axis=0, keepdims=True), axis=1, keepdims=True)
     energy = energy * (0.5 / ATOMS)
-    back = dot3(table_xt, split(scaled))
-    wide_ref[...] = dot3(split(back), table_y, ((1,), (1,)))
-    for y in range(PAD_Y):
-        for h in range(2):
-            block = jnp.zeros((ROW_X, 128), F32)
-            for s in range(4):
-                g = 4 * h + s
-                piece = wide_ref[
-                    ROW_X * g : ROW_X * (g + 1), 128 * (y // 4) : 128 * (y // 4) + 128
-                ]
-                shift = (32 * (s - y % 4)) % 128
-                if shift:
-                    piece = pltpu.roll(piece, shift, 1)
-                block = jnp.where(section == s, piece, block)
-            turned_ref[h, pl.ds(y, PAD_X, stride=PAD_Y), :] = block[:PAD_X]
-    lane = iota((256, 128), 1)
+    back = dot3(table, split(scaled))
+    wide_ref[...] = dot3(split(back), order, ((1,), (1,)))
     for h in range(2):
+        for quad in range(2):
+            columns = slice(128 * quad, 128 * quad + 128)
+            pieces = []
+            for g in range(4 * h, 4 * h + 4):
+                after = BLOCK_X * ((g + 1) % N_GRP)
+                pieces.append(
+                    jnp.concatenate(
+                        [
+                            wide_ref[BLOCK_X * g : BLOCK_X * (g + 1), columns],
+                            wide_ref[after : after + 8, columns],
+                        ],
+                        axis=0,
+                    )
+                )
+            for i in range(4):
+                y = 4 * quad + i
+                block = regroup(pieces, i, section)
+                turned_ref[h, pl.ds(y, PAD_X, stride=PAD_Y), :] = block[:PAD_X]
+                if y < PAD_Y - BLOCK_Y:
+                    block = to_previous(block, place)
+                    rows = pl.ds(y + BLOCK_Y, PAD_X, stride=PAD_Y)
+                    turned_ref[h, rows, :] = block[:PAD_X]
         turned_ref[h, USED:CHUNK, :] = jnp.zeros((CHUNK - USED, 128), F32)
+    spot = iota((256, 128), 1) == USED - 384
     for j in range(4):
         rows = slice(128 * j, 128 * j + 128)
         block = jnp.concatenate([turned_ref[0, rows, :], turned_ref[1, rows, :]], axis=1).T
         if j == 3:
-            block = jnp.where(lane == USED - 384, energy, block)
+            block = jnp.where(spot, energy, block)
         out_ref[pl.ds(j, 256, stride=4), :] = block
 
 
 def force_kernel(
-    offsets_ref, cell_z_ref, frac_ref, live_ref, in_ref, high_ref, low_ref, forces_ref, energy_ref,
-    packed_ref, mesh_high_ref, mesh_low_ref,
+    offsets_ref, cell_z_ref, frac_ref, live_ref, in_ref, table_ref, forces_ref, energy_ref,
+    packed_ref, mesh_ref, mesh_high_ref, mesh_low_ref,
 ):
-    table = (high_ref[...], low_ref[...])
+    table = (table_ref[:K, :], table_ref[K:, :])
     lane = iota((256, 128), 1)
     for j in range(4):
         chunk = in_ref[pl.ds(j, 256, stride=4), :]
@@ -283,11 +308,10 @@
             )
         packed_ref[128 * j : 128 * j + 128, :] = dot3(split(chunk.T), table)
     for x in range(PAD_X):
-        high, low = split(packed_ref[PAD_Y * x : PAD_Y * x + 16, :])
-        mesh_high_ref[16 * x : 16 * x + 16, :] = high
-        mesh_low_ref[16 * x : 16 * x + 16, :] = low
-    mesh_high_ref[16 * PAD_X :, :] = jnp.zeros((ROWS - 16 * PAD_X, 256), BF16)
-    mesh_low_ref[16 * PAD_X :, :] = jnp.zeros((ROWS - 16 * PAD_X, 256), BF16)
+        mesh_ref[16 * x : 16 * x + 16, :] = packed_ref[PAD_Y * x : PAD_Y * x + 16, :]
+    high, low = split(mesh_ref[...])
+    mesh_high_ref[...] = high
+    mesh_low_ref[...] = low
 
     @pl.loop(0, TILES_X // GROUP)
     def _(group):
@@ -301,14 +325,14 @@
             grade_x = pick(from_x, grades[0])
             weight_y = pick(from_y, rows[1])
             grade_y = pick(from_y, grades[1])
-            place = pl.ds(pl.multiple_of(column * 32, 32), 128)
+            place = pl.ds(pl.multiple_of(column * 32, 32), 112)
             footing = (mesh_high_ref[place, :], mesh_low_ref[place, :])
             main = dot3(footing, along_z(from_z, owner_z, rows[2]))
             tilt = dot3(footing, along_z(from_z, owner_z, grades[2]))
             sum_x = 0.0
             sum_y = 0.0
             sum_z = 0.0
-            for i in range(8):
+            for i in range(7):
                 band = main[16 * i : 16 * i + 16, :]
                 sum_x = sum_x + grade_x[i : i + 1, :] * band
                 sum_y = sum_y + weight_x[i : i + 1, :] * band
@@ -339,9 +363,9 @@
     slots = charges.shape[0]
     cell_z = cell_z.reshape(1, slots)
     charges = charges.reshape(1, slots)
-    table = [jnp.asarray(value) for value in TABLES["full"]]
+    table = jnp.asarray(TABLES["full"])
     block = jax.ShapeDtypeStruct((1024, 128), F32)
-    sources = [tile_counts, cell_offsets, cell_z, frac, charges, *table]
+    sources = [tile_counts, cell_offsets, cell_z, frac, charges, table]
     outgoing, live_q = call(
         spread_kernel,
         (block, jax.ShapeDtypeStruct((1, slots), F32)),
@@ -359,9 +383,11 @@
     returning = call(
         plane_kernel,
         block,
-        [pltpu.VMEM((2, CHUNK + SPARE, 128), F32), pltpu.VMEM((N_GRP * ROW_X, CHUNK), F32)],
+        [pltpu.VMEM((2, CHUNK + SPARE, 128), F32), pltpu.VMEM((K, K), F32)],
         plane,
-        *[jnp.asarray(TABLES[name]) for name in ("plane", "wide", "x")],
+        jnp.asarray(TABLES["plane"]),
+        jnp.asarray(TABLES["order"]),
+        table,
     )
     home = exchange(returning)
     forces, energy = call(
@@ -369,6 +395,7 @@
         (jax.ShapeDtypeStruct((3, slots), F32), jax.ShapeDtypeStruct((1, 1), F32)),
         [
             pltpu.VMEM((CHUNK, 256), F32),
+            pltpu.VMEM((ROWS, 256), F32),
             pltpu.VMEM((ROWS, 256), BF16),
             pltpu.VMEM((ROWS, 256), BF16),
         ],
@@ -377,7 +404,7 @@
         frac,
         live_q,
         home,
-        *table,
+        table,
     )
     return forces, energy.reshape(())
 

time: 71.6 us -> 70.8 us (0.989)
  Pallas kernels: 9.42 us -> 8.66 us
    pallas_call x3, Pallas kernels: 9.42 us -> 8.66 us  [call(): pl.pallas_call(kernel, out_shape=out_shape, in_specs=[pl.BlockSpec(memory...]
where the time goes in v5:
time: 70.8 us; the launch traced here: 70.6 us
  blocking collectives  61.2 us (86%)
  Pallas kernels  8.66 us (12%)
    all_to_all x2, blocking collectives, exchange(): lax.all_to_all(block.reshape(256, 4, 128), AXES, 0, 0, tiled=True)  61.2 us
    pallas_call x3, Pallas kernels, call(): pl.pallas_call(kernel, out_shape=out_shape, in_specs=[pl.BlockSpec(memory...  8.66 us

profile of v5, /device:TPU:1, one launch (start us, length us, event | category | flops | bytes accessed | tf_op | source)
XLA Modules:
  0.0 70.6 jit_solution(9508928128698731364)
XLA Ops:
  0.6 0.0 copy-start.5
  0.6 3.3 %shard_map.95 = (f32[1024,128]{1,0:T(8,128)S(1)}, f32[1,4096]{1,0:T(1,128)S(1)}) custom-call(s32[64]{0:T(128)} %counts_hbm.1, s32[2,4096]{1,0:T(2,128)} %offsets_ref.1, s32[1,4096]{1,0:T(1,128)} %bitcast.11, f32[3,4096]{1,0:T(4,128)} %frac_ref.1, f32[1,4096]{1,0:T(1,128)} %bitcast.13, bf16[512,256]{1,0:T(8,128)(2,1)} %constant.6.clone.table_hbm.table_ref), custom_call_target="tpu_custom_call" | custom-call | flops 3000000000 | bytes 10000000 | tf_op jit(solution)/shard_map/pallas_call | solution.py:347
  3.9 0.0 copy-start.3
  4.0 0.0 copy-start.4
  4.0 35.3 %all_to_all.10 = f32[256,4,128]{2,1,0:T(4,128)S(1)} all-to-all(f32[256,4,128]{2,1,0:T(4,128)S(1)} %bitcast.10), channel_id=1, replica_groups=mesh['grp'=8,'pen'=32] {'grp','pen'}, dimensions={0} | all-to-all | bytes 1048576 | tf_op jit(solution)/shard_map/all_to_all | solution.py:359
  39.3 0.0 copy-done.5
  39.3 0.0 copy-done.3
  39.3 0.0 copy-done.4
  39.3 2.2 %shard_map.96 = f32[1024,128]{1,0:T(8,128)S(1)} custom-call(f32[1024,128]{1,0:T(8,128)S(1)} %bitcast.8, f32[514,256]{1,0:T(8,128)S(1)} %copy-done.3, bf16[512,256]{1,0:T(8,128)(2,1)S(1)} %copy-done.5, bf16[512,256]{1,0:T(8,128)(2,1)S(1)} %copy-done.4), custom_call_target="tpu_custom_call" | custom-call | flops 3000000000 | bytes 10000000 | tf_op jit(solution)/shard_map/pallas_call | solution.py:347
  41.6 0.0 copy-start
  41.6 0.0 copy-start.1
  41.6 0.0 copy-start.2
  41.6 25.9 %all_to_all.11 = f32[256,4,128]{2,1,0:T(4,128)S(1)} all-to-all(f32[256,4,128]{2,1,0:T(4,128)S(1)} %bitcast.9), channel_id=1, replica_groups=mesh['grp'=8,'pen'=32] {'grp','pen'}, dimensions={0} | all-to-all | bytes 1048576 | tf_op jit(solution)/shard_map/all_to_all | solution.py:359
  67.5 0.0 copy-done
  67.5 0.0 copy-done.1
  67.5 0.0 copy-done.2
  67.5 3.1 %shard_map.97 = (f32[3,4096]{1,0:T(4,128)}, f32[1,1]{1,0:T(1,128)}) custom-call(s32[2,4096]{1,0:T(2,128)S(1)} %copy-done.1, s32[1,4096]{1,0:T(1,128)S(1)} %bitcast.12, f32[3,4096]{1,0:T(4,128)S(1)} %copy-done, f32[1,4096]{1,0:T(1,128)S(1)} %get-tuple-element.6.live_ref, f32[1024,128]{1,0:T(8,128)S(1)} %bitcast.7, bf16[512,256]{1,0:T(8,128)(2,1)S(1)} %copy-done.4), custom_call_target="tpu_custom_call" | custom-call | flops 3000000000 | bytes 10000000 | tf_op jit(solution)/shard_map/pallas_call | solution.py:347
Async XLA Ops:
  0.6 38.7 %copy-start.5 = (bf16[512,256]{1,0:T(8,128)(2,1)S(1)}, bf16[512,256]{1,0:T(8,128)(2,1)}, u32[]{:S(2)}) copy-start(bf16[512,256]{1,0:T(8,128)(2,1)} %constant.8.clone.order_ref) | copy-start | bytes 786436
  3.9 35.4 %copy-start.3 = (f32[514,256]{1,0:T(8,128)S(1)}, f32[514,256]{1,0:T(8,128)}, u32[]{:S(2)}) copy-start(f32[514,256]{1,0:T(8,128)} %constant.7.clone.plane_ref) | copy-start | bytes 1579012
  4.0 35.4 %copy-start.4 = (bf16[512,256]{1,0:T(8,128)(2,1)S(1)}, bf16[512,256]{1,0:T(8,128)(2,1)}, u32[]{:S(2)}) copy-start(bf16[512,256]{1,0:T(8,128)(2,1)} %constant.6.clone.table_hbm.table_ref) | copy-start | bytes 786436
  41.6 25.9 %copy-start = (f32[3,4096]{1,0:T(4,128)S(1)}, f32[3,4096]{1,0:T(4,128)}, u32[]{:S(2)}) copy-start(f32[3,4096]{1,0:T(4,128)} %frac_ref.1) | copy-start | bytes 147460
  41.6 25.9 %copy-start.1 = (s32[2,4096]{1,0:T(2,128)S(1)}, s32[2,4096]{1,0:T(2,128)}, u32[]{:S(2)}) copy-start(s32[2,4096]{1,0:T(2,128)} %offsets_ref.1) | copy-start | bytes 98308
  41.6 25.9 %copy-start.2 = (s32[4096]{0:T(1024)S(1)}, s32[4096]{0:T(1024)}, u32[]{:S(2)}) copy-start(s32[4096]{0:T(1024)} %param.9) | copy-start | bytes 49156

commit v6 on v5

--- a/solution.py
+++ b/solution.py
@@ -25,7 +25,6 @@
 ROWS = 16 * PAD_X
 ROW_X = 40
 SPARE = 16
-GROUP = 16
 F32 = jnp.float32
 BF16 = jnp.bfloat16
 
@@ -120,33 +119,25 @@
 
 
 def column_lanes(column):
-    return pl.ds(pl.multiple_of(column * 256, 256), 256)
-
-
-def group_splines(group, frac_ref):
-    fracs = [frac_ref[:, column_lanes(GROUP * group + c)] for c in range(GROUP)]
+    return slice(256 * column, 256 * column + 256)
+
+
+def group_splines(frac_ref):
+    fracs = [frac_ref[:, column_lanes(column)] for column in range(TILES_X)]
     return spline_rows(jnp.concatenate(fracs, axis=0))
 
 
-def column_parts(group, c, splines, offsets_ref, cell_z_ref):
-    column = GROUP * group + c
+def column_parts(column, offsets_ref, cell_z_ref):
     lanes = column_lanes(column)
-    rows, grades = [
-        [[value[3 * c + d : 3 * c + d + 1, :] for value in values] for d in range(3)]
-        for values in splines
-    ]
     tile = iota((1, 256), 1) // 64
     from_x = iota((8, 256), 0) - offsets_ref[0:1, lanes]
     from_y = iota((16, 256), 0) - (offsets_ref[1:2, lanes] + 2 * tile)
-    cell_z = cell_z_ref[:, lanes]
-    from_z = (iota((16, 256), 0) - cell_z) & 15
-    owner_z = (((cell_z + from_z) & (K - 1)) >> 4).astype(F32).astype(BF16)
-    return column, lanes, rows, grades, from_x, from_y, from_z, owner_z
-
-
-def along_z(from_z, owner_z, rows):
+    from_z = (iota((16, 256), 0) - cell_z_ref[:, lanes]) & 15
+    return lanes, from_x, from_y, from_z
+
+
+def blocks_z(owner_z, parts):
     zero = jnp.zeros((16, 256), BF16)
-    parts = split(pick(from_z, rows))
     return tuple(
         jnp.concatenate([jnp.where(owner_z == float(h), part, zero) for h in range(16)], axis=0)
         for part in parts
@@ -155,7 +146,7 @@
 
 def spread_kernel(
     counts_hbm, offsets_hbm, cell_z_hbm, frac_hbm, charges_hbm, table_hbm, out_ref, live_ref,
-    mesh_ref, packed_ref, counts_ref, offsets_ref, cell_z_ref, frac_ref, charges_ref, table_ref,
+    slopes_ref, owner_ref, high_z_ref, low_z_ref, weight_x_ref, weight_y_ref, mesh_ref, packed_ref, counts_ref, offsets_ref, cell_z_ref, frac_ref, charges_ref, table_ref,
     sems,
 ):
     sources = [counts_hbm, offsets_hbm, cell_z_hbm, frac_hbm, charges_hbm, table_hbm]
@@ -167,37 +158,52 @@
     for copy in copies:
         copy.start()
     mesh_ref[...] = jnp.zeros_like(mesh_ref)
-    for copy in copies[:5]:
+    for copy in copies:
         copy.wait()
 
-    @pl.loop(0, TILES_X // GROUP)
-    def _(group):
-        splines = group_splines(group, frac_ref)
-        for c in range(GROUP):
-            column, lanes, rows, grades, from_x, from_y, from_z, owner_z = column_parts(
-                group, c, splines, offsets_ref, cell_z_ref
-            )
-            lane = iota((1, 256), 1)
-            counts = jnp.full((1, 256), counts_ref[4 * column], jnp.int32)
-            for b in range(1, 4):
-                counts = jnp.where(lane // 64 == b, counts_ref[4 * column + b], counts)
-            live_q = jnp.where(lane % 64 < counts, charges_ref[:, lanes], 0.0)
-            live_ref[:, lanes] = live_q
-            weight_x = pick(from_x, rows[0]) * live_q
-            weight_y = pick(from_y, rows[1])
-            pair = jnp.concatenate([weight_x[i : i + 1, :] * weight_y for i in range(7)], axis=0)
-            weight_z = along_z(from_z, owner_z, rows[2])
-            place = pl.ds(pl.multiple_of(column * 32, 32), 112)
-            mesh_ref[place, :] += dot3(split(pair), weight_z, ((1,), (1,)))
-
-    for x in range(PAD_X):
-        packed_ref[PAD_Y * x : PAD_Y * (x + 1), :] = mesh_ref[16 * x : 16 * x + PAD_Y, :]
-    packed_ref[USED:, :] = jnp.zeros((CHUNK - USED, 256), F32)
-    for copy in copies[5:]:
-        copy.wait()
-    spectrum = dot3((table_ref[:K, :], table_ref[K:, :]), split(packed_ref[...]), ((1,), (1,)))
-    for j in range(4):
-        out_ref[pl.ds(j, 256, stride=4), :] = spectrum[:, 128 * j : 128 * j + 128]
+    def pack(first, end):
+        for x in range(first, end):
+            packed_ref[PAD_Y * x : PAD_Y * (x + 1), :] = mesh_ref[16 * x : 16 * x + PAD_Y, :]
+
+    def transform(first):
+        section = split(packed_ref[first : first + 256, :])
+        spectrum = dot3((table_ref[:K, :], table_ref[K:, :]), section, ((1,), (1,)))
+        for j in range(2):
+            out_ref[pl.ds(first // 128 + j, 256, stride=4), :] = spectrum[:, 128 * j : 128 * j + 128]
+
+    values, slopes = group_splines(frac_ref)
+    for j in range(6):
+        slopes_ref[48 * j : 48 * j + 48, :] = slopes[j]
+    for column in range(TILES_X):
+        lanes, from_x, from_y, from_z = column_parts(column, offsets_ref, cell_z_ref)
+        rows = [
+            [value[3 * column + d : 3 * column + d + 1, :] for value in values] for d in range(3)
+        ]
+        owner_z = (((cell_z_ref[:, lanes] + from_z) & (K - 1)) >> 4).astype(F32).astype(BF16)
+        lane = iota((1, 256), 1)
+        counts = jnp.full((1, 256), counts_ref[4 * column], jnp.int32)
+        for b in range(1, 4):
+            counts = jnp.where(lane // 64 == b, counts_ref[4 * column + b], counts)
+        live_q = jnp.where(lane % 64 < counts, charges_ref[:, lanes], 0.0)
+        live_ref[:, lanes] = live_q
+        weight_x = pick(from_x, rows[0]) * live_q
+        weight_y = pick(from_y, rows[1])
+        pair = jnp.concatenate([weight_x[i : i + 1, :] * weight_y for i in range(7)], axis=0)
+        parts_z = split(pick(from_z, rows[2]))
+        owner_ref[:, lanes] = owner_z
+        high_z_ref[:, lanes], low_z_ref[:, lanes] = parts_z
+        weight_x_ref[:, lanes] = weight_x
+        weight_y_ref[:, lanes] = weight_y
+        weight_z = blocks_z(owner_z, parts_z)
+        place = slice(32 * column, 32 * column + 112)
+        mesh_ref[place, :] += dot3(split(pair), weight_z, ((1,), (1,)))
+        if column == 9:
+            pack(0, 20)
+            transform(0)
+
+    packed_ref[USED:CHUNK, :] = jnp.zeros((CHUNK - USED, 256), F32)
+    pack(20, PAD_X)
+    transform(256)
 
 
 def regroup(pieces, own, section):
@@ -294,7 +300,8 @@
 
 
 def force_kernel(
-    offsets_ref, cell_z_ref, frac_ref, live_ref, in_ref, table_ref, forces_ref, energy_ref,
+    offsets_ref, cell_z_ref, live_ref, slopes_ref, owner_ref, high_z_ref, low_z_ref, weight_x_ref,
+    weight_y_ref, in_ref, table_ref, forces_ref, energy_ref,
     packed_ref, mesh_ref, mesh_high_ref, mesh_low_ref,
 ):
     table = (table_ref[:K, :], table_ref[K:, :])
@@ -313,33 +320,31 @@
     mesh_high_ref[...] = high
     mesh_low_ref[...] = low
 
-    @pl.loop(0, TILES_X // GROUP)
-    def _(group):
-        splines = group_splines(group, frac_ref)
-        for c in range(GROUP):
-            column, lanes, rows, grades, from_x, from_y, from_z, owner_z = column_parts(
-                group, c, splines, offsets_ref, cell_z_ref
-            )
-            live_q = live_ref[:, lanes]
-            weight_x = pick(from_x, rows[0])
-            grade_x = pick(from_x, grades[0])
-            weight_y = pick(from_y, rows[1])
-            grade_y = pick(from_y, grades[1])
-            place = pl.ds(pl.multiple_of(column * 32, 32), 112)
-            footing = (mesh_high_ref[place, :], mesh_low_ref[place, :])
-            main = dot3(footing, along_z(from_z, owner_z, rows[2]))
-            tilt = dot3(footing, along_z(from_z, owner_z, grades[2]))
-            sum_x = 0.0
-            sum_y = 0.0
-            sum_z = 0.0
-            for i in range(7):
-                band = main[16 * i : 16 * i + 16, :]
-                sum_x = sum_x + grade_x[i : i + 1, :] * band
-                sum_y = sum_y + weight_x[i : i + 1, :] * band
-                sum_z = sum_z + weight_x[i : i + 1, :] * tilt[16 * i : 16 * i + 16, :]
-            forces_ref[0:1, lanes] = -live_q * jnp.sum(weight_y * sum_x, axis=0, keepdims=True)
-            forces_ref[1:2, lanes] = -live_q * jnp.sum(grade_y * sum_y, axis=0, keepdims=True)
-            forces_ref[2:3, lanes] = -live_q * jnp.sum(weight_y * sum_z, axis=0, keepdims=True)
+    for column in range(TILES_X):
+        lanes, from_x, from_y, from_z = column_parts(column, offsets_ref, cell_z_ref)
+        spots = [[48 * j + 3 * column + d for j in range(6)] for d in range(3)]
+        grades = [[slopes_ref[spot : spot + 1, :] for spot in line] for line in spots]
+        owner_z = owner_ref[:, lanes]
+        weight_x = weight_x_ref[:, lanes]
+        weight_y = weight_y_ref[:, lanes]
+        live_q = live_ref[:, lanes]
+        grade_x = pick(from_x, grades[0])
+        grade_y = pick(from_y, grades[1])
+        place = slice(32 * column, 32 * column + 112)
+        footing = (mesh_high_ref[place, :], mesh_low_ref[place, :])
+        main = dot3(footing, blocks_z(owner_z, (high_z_ref[:, lanes], low_z_ref[:, lanes])))
+        tilt = dot3(footing, blocks_z(owner_z, split(pick(from_z, grades[2]))))
+        sum_x = 0.0
+        sum_y = 0.0
+        sum_z = 0.0
+        for i in range(7):
+            band = main[16 * i : 16 * i + 16, :]
+            sum_x = sum_x + grade_x[i : i + 1, :] * band
+            sum_y = sum_y + weight_x[i : i + 1, :] * band
+            sum_z = sum_z + weight_x[i : i + 1, :] * tilt[16 * i : 16 * i + 16, :]
+        forces_ref[0:1, lanes] = -live_q * jnp.sum(weight_y * sum_x, axis=0, keepdims=True)
+        forces_ref[1:2, lanes] = -jnp.sum(grade_y * sum_y, axis=0, keepdims=True)
+        forces_ref[2:3, lanes] = -jnp.sum(weight_y * sum_z, axis=0, keepdims=True)
 
 
 def call(kernel, out_shape, scratch, *args, memory=pltpu.VMEM):
@@ -366,9 +371,18 @@
     table = jnp.asarray(TABLES["full"])
     block = jax.ShapeDtypeStruct((1024, 128), F32)
     sources = [tile_counts, cell_offsets, cell_z, frac, charges, table]
-    outgoing, live_q = call(
+    outgoing, *kept = call(
         spread_kernel,
-        (block, jax.ShapeDtypeStruct((1, slots), F32)),
+        (
+            block,
+            jax.ShapeDtypeStruct((1, slots), F32),
+            jax.ShapeDtypeStruct((6 * 3 * TILES_X, 256), F32),
+            jax.ShapeDtypeStruct((16, slots), BF16),
+            jax.ShapeDtypeStruct((16, slots), BF16),
+            jax.ShapeDtypeStruct((16, slots), BF16),
+            jax.ShapeDtypeStruct((8, slots), F32),
+            jax.ShapeDtypeStruct((16, slots), F32),
+        ),
         [
             pltpu.VMEM((ROWS, 256), F32),
             pltpu.VMEM((CHUNK, 256), F32),
@@ -401,8 +415,7 @@
         ],
         cell_offsets,
         cell_z,
-        frac,
-        live_q,
+        *kept,
         home,
         table,
     )

time: 70.8 us -> 70.5 us (level)
  no operation moved by 1% of the time
where the time goes in v6:
time: 70.5 us; the launch traced here: 70.3 us
  blocking collectives  61.2 us (87%)
  Pallas kernels  8.38 us (12%)
    all_to_all x2, blocking collectives, exchange(): lax.all_to_all(block.reshape(256, 4, 128), AXES, 0, 0, tiled=True)  61.2 us
    pallas_call x3, Pallas kernels, call(): pl.pallas_call(kernel, out_shape=out_shape, in_specs=[pl.BlockSpec(memory...  8.38 us

profile of v6, /device:TPU:1, one launch (start us, length us, event | category | flops | bytes accessed | tf_op | source)
XLA Modules:
  0.0 70.3 jit_solution(15570532131300506850)
XLA Ops:
  0.6 0.0 copy-start.4
  0.6 3.2 %shard_map.95 = (f32[1024,128]{1,0:T(8,128)S(1)}, f32[1,4096]{1,0:T(1,128)S(1)}, f32[288,256]{1,0:T(8,128)S(1)}, bf16[16,4096]{1,0:T(8,128)(2,1)S(1)}, bf16[16,4...) custom-call(s32[64]{0:T(128)} %counts_hbm.1, ...), custom_call_target="tpu_custom_call" | custom-call | flops 3000000000 | bytes 10000000 | tf_op jit(solution)/shard_map/pallas_call | solution.py:352
  3.9 0.0 copy-start.2
  3.9 0.0 copy-start.3
  3.9 35.3 %all_to_all.10 = f32[256,4,128]{2,1,0:T(4,128)S(1)} all-to-all(f32[256,4,128]{2,1,0:T(4,128)S(1)} %bitcast.8), channel_id=1, replica_groups=mesh['grp'=8,'pen'=32] {'grp','pen'}, dimensions={0} | all-to-all | bytes 1048576 | tf_op jit(solution)/shard_map/all_to_all | solution.py:364
  39.2 0.0 copy-done.4
  39.2 0.0 copy-done.2
  39.2 0.0 copy-done.3
  39.2 2.2 %shard_map.96 = f32[1024,128]{1,0:T(8,128)S(1)} custom-call(f32[1024,128]{1,0:T(8,128)S(1)} %bitcast.9, f32[514,256]{1,0:T(8,128)S(1)} %copy-done.2, bf16[512,256]{1,0:T(8,128)(2,1)S(1)} %copy-done.4, bf16[512,256]{1,0:T(8,128)(2,1)S(1)} %copy-done.3), custom_call_target="tpu_custom_call" | custom-call | flops 3000000000 | bytes 10000000 | tf_op jit(solution)/shard_map/pallas_call | solution.py:352
  41.5 0.0 copy-start
  41.5 0.0 copy-start.1
  41.5 25.9 %all_to_all.11 = f32[256,4,128]{2,1,0:T(4,128)S(1)} all-to-all(f32[256,4,128]{2,1,0:T(4,128)S(1)} %bitcast.10), channel_id=1, replica_groups=mesh['grp'=8,'pen'=32] {'grp','pen'}, dimensions={0} | all-to-all | bytes 1048576 | tf_op jit(solution)/shard_map/all_to_all | solution.py:364
  67.4 0.0 copy-done
  67.4 0.0 copy-done.1
  67.4 2.9 %shard_map.97 = (f32[3,4096]{1,0:T(4,128)}, f32[1,1]{1,0:T(1,128)}) custom-call(s32[2,4096]{1,0:T(2,128)S(1)} %copy-done, s32[1,4096]{1,0:T(1,128)S(1)} %bitcast.12, f32[1,4096]{1,0:T(1,128)S(1)} %get-tuple-element.12.live_ref, f32[288,256]{1,0:T(8,128)S(1)} %get-tuple-element.13.slopes_ref, bf16[16,4096]{1,0:T(8,128)(2,1)S(1)} %get-tuple-element.14.owner_ref, ...), custom_call_target="tpu_custom_call" | custom-call | flops 3000000000 | bytes 10000000 | tf_op jit(solution)/shard_map/pallas_call | solution.py:352
Async XLA Ops:
  0.6 38.6 %copy-start.4 = (bf16[512,256]{1,0:T(8,128)(2,1)S(1)}, bf16[512,256]{1,0:T(8,128)(2,1)}, u32[]{:S(2)}) copy-start(bf16[512,256]{1,0:T(8,128)(2,1)} %constant.8.clone.order_ref) | copy-start | bytes 786436
  3.9 35.4 %copy-start.2 = (f32[514,256]{1,0:T(8,128)S(1)}, f32[514,256]{1,0:T(8,128)}, u32[]{:S(2)}) copy-start(f32[514,256]{1,0:T(8,128)} %constant.7.clone.plane_ref) | copy-start | bytes 1579012
  3.9 35.4 %copy-start.3 = (bf16[512,256]{1,0:T(8,128)(2,1)S(1)}, bf16[512,256]{1,0:T(8,128)(2,1)}, u32[]{:S(2)}) copy-start(bf16[512,256]{1,0:T(8,128)(2,1)} %constant.6.clone.table_hbm.table_ref) | copy-start | bytes 786436
  41.5 25.9 %copy-start = (s32[2,4096]{1,0:T(2,128)S(1)}, s32[2,4096]{1,0:T(2,128)}, u32[]{:S(2)}) copy-start(s32[2,4096]{1,0:T(2,128)} %offsets_ref.1) | copy-start | bytes 98308
  41.5 25.9 %copy-start.1 = (s32[4096]{0:T(1024)S(1)}, s32[4096]{0:T(1024)}, u32[]{:S(2)}) copy-start(s32[4096]{0:T(1024)} %param.9) | copy-start | bytes 49156

commit v7 on v6

--- a/solution.py
+++ b/solution.py
@@ -146,7 +146,7 @@
 
 def spread_kernel(
     counts_hbm, offsets_hbm, cell_z_hbm, frac_hbm, charges_hbm, table_hbm, out_ref, live_ref,
-    slopes_ref, owner_ref, high_z_ref, low_z_ref, weight_x_ref, weight_y_ref, mesh_ref, packed_ref, counts_ref, offsets_ref, cell_z_ref, frac_ref, charges_ref, table_ref,
+    slopes_ref, owner_ref, taps_z_ref, weight_x_ref, weight_y_ref, mesh_ref, packed_ref, counts_ref, offsets_ref, cell_z_ref, frac_ref, charges_ref, table_ref,
     sems,
 ):
     sources = [counts_hbm, offsets_hbm, cell_z_hbm, frac_hbm, charges_hbm, table_hbm]
@@ -179,7 +179,7 @@
         rows = [
             [value[3 * column + d : 3 * column + d + 1, :] for value in values] for d in range(3)
         ]
-        owner_z = (((cell_z_ref[:, lanes] + from_z) & (K - 1)) >> 4).astype(F32).astype(BF16)
+        owner_z = (((cell_z_ref[:, lanes] + from_z) & (K - 1)) >> 4).astype(F32)
         lane = iota((1, 256), 1)
         counts = jnp.full((1, 256), counts_ref[4 * column], jnp.int32)
         for b in range(1, 4):
@@ -189,12 +189,12 @@
         weight_x = pick(from_x, rows[0]) * live_q
         weight_y = pick(from_y, rows[1])
         pair = jnp.concatenate([weight_x[i : i + 1, :] * weight_y for i in range(7)], axis=0)
-        parts_z = split(pick(from_z, rows[2]))
+        taps_z = pick(from_z, rows[2])
         owner_ref[:, lanes] = owner_z
-        high_z_ref[:, lanes], low_z_ref[:, lanes] = parts_z
+        taps_z_ref[:, lanes] = taps_z
         weight_x_ref[:, lanes] = weight_x
         weight_y_ref[:, lanes] = weight_y
-        weight_z = blocks_z(owner_z, parts_z)
+        weight_z = blocks_z(owner_z.astype(BF16), split(taps_z))
         place = slice(32 * column, 32 * column + 112)
         mesh_ref[place, :] += dot3(split(pair), weight_z, ((1,), (1,)))
         if column == 9:
@@ -300,7 +300,7 @@
 
 
 def force_kernel(
-    offsets_ref, cell_z_ref, live_ref, slopes_ref, owner_ref, high_z_ref, low_z_ref, weight_x_ref,
+    offsets_ref, cell_z_ref, live_ref, slopes_ref, owner_ref, taps_z_ref, weight_x_ref,
     weight_y_ref, in_ref, table_ref, forces_ref, energy_ref,
     packed_ref, mesh_ref, mesh_high_ref, mesh_low_ref,
 ):
@@ -324,7 +324,7 @@
         lanes, from_x, from_y, from_z = column_parts(column, offsets_ref, cell_z_ref)
         spots = [[48 * j + 3 * column + d for j in range(6)] for d in range(3)]
         grades = [[slopes_ref[spot : spot + 1, :] for spot in line] for line in spots]
-        owner_z = owner_ref[:, lanes]
+        owner_z = owner_ref[:, lanes].astype(BF16)
         weight_x = weight_x_ref[:, lanes]
         weight_y = weight_y_ref[:, lanes]
         live_q = live_ref[:, lanes]
@@ -332,7 +332,7 @@
         grade_y = pick(from_y, grades[1])
         place = slice(32 * column, 32 * column + 112)
         footing = (mesh_high_ref[place, :], mesh_low_ref[place, :])
-        main = dot3(footing, blocks_z(owner_z, (high_z_ref[:, lanes], low_z_ref[:, lanes])))
+        main = dot3(footing, blocks_z(owner_z, split(taps_z_ref[:, lanes])))
         tilt = dot3(footing, blocks_z(owner_z, split(pick(from_z, grades[2]))))
         sum_x = 0.0
         sum_y = 0.0
@@ -377,9 +377,8 @@
             block,
             jax.ShapeDtypeStruct((1, slots), F32),
             jax.ShapeDtypeStruct((6 * 3 * TILES_X, 256), F32),
-            jax.ShapeDtypeStruct((16, slots), BF16),
-            jax.ShapeDtypeStruct((16, slots), BF16),
-            jax.ShapeDtypeStruct((16, slots), BF16),
+            jax.ShapeDtypeStruct((16, slots), F32),
+            jax.ShapeDtypeStruct((16, slots), F32),
             jax.ShapeDtypeStruct((8, slots), F32),
             jax.ShapeDtypeStruct((16, slots), F32),
         ),

time: 70.5 us -> 70.3 us (level)
  no operation moved by 1% of the time
where the time goes in v7:
time: 70.3 us; the launch traced here: 70.1 us
  blocking collectives  61.2 us (87%)
  Pallas kernels  8.17 us (12%)
    all_to_all x2, blocking collectives, exchange(): lax.all_to_all(block.reshape(256, 4, 128), AXES, 0, 0, tiled=True)  61.2 us
    pallas_call x3, Pallas kernels, call(): pl.pallas_call(kernel, out_shape=out_shape, in_specs=[pl.BlockSpec(memory...  8.17 us

profile of v7, /device:TPU:1, one launch (start us, length us, event | category | flops | bytes accessed | tf_op | source)
XLA Modules:
  0.0 70.1 jit_solution(9757550139638099697)
XLA Ops:
  0.6 0.0 copy-start.4
  0.6 3.2 %shard_map.95 = (f32[1024,128]{1,0:T(8,128)S(1)}, f32[1,4096]{1,0:T(1,128)S(1)}, f32[288,256]{1,0:T(8,128)S(1)}, f32[16,4096]{1,0:T(8,128)S(1)}, f32[16,4096]{1,...) custom-call(s32[64]{0:T(128)} %counts_hbm.1, s32[2,4096]{1,0:T(2,128)} %offsets_ref.1, s32[1,4096]{1,0:T(1,128)} %bitcast.11, ...), custom_call_target="tpu_custom_call" | custom-call | flops 3000000000 | bytes 10000000 | tf_op jit(solution)/shard_map/pallas_call | solution.py:352
  3.9 0.0 copy-start.2
  3.9 0.0 copy-start.3
  3.9 35.3 %all_to_all.10 = f32[256,4,128]{2,1,0:T(4,128)S(1)} all-to-all(f32[256,4,128]{2,1,0:T(4,128)S(1)} %bitcast.8), channel_id=1, replica_groups=mesh['grp'=8,'pen'=32] {'grp','pen'}, dimensions={0} | all-to-all | bytes 1048576 | tf_op jit(solution)/shard_map/all_to_all | solution.py:364
  39.2 0.0 copy-done.4
  39.2 0.0 copy-done.2
  39.2 0.0 copy-done.3
  39.2 2.2 %shard_map.96 = f32[1024,128]{1,0:T(8,128)S(1)} custom-call(f32[1024,128]{1,0:T(8,128)S(1)} %bitcast.9, f32[514,256]{1,0:T(8,128)S(1)} %copy-done.2, bf16[512,256]{1,0:T(8,128)(2,1)S(1)} %copy-done.4, bf16[512,256]{1,0:T(8,128)(2,1)S(1)} %copy-done.3), custom_call_target="tpu_custom_call" | custom-call | flops 3000000000 | bytes 10000000 | tf_op jit(solution)/shard_map/pallas_call | solution.py:352
  41.5 0.0 copy-start
  41.5 0.0 copy-start.1
  41.5 25.9 %all_to_all.11 = f32[256,4,128]{2,1,0:T(4,128)S(1)} all-to-all(f32[256,4,128]{2,1,0:T(4,128)S(1)} %bitcast.10), channel_id=1, replica_groups=mesh['grp'=8,'pen'=32] {'grp','pen'}, dimensions={0} | all-to-all | bytes 1048576 | tf_op jit(solution)/shard_map/all_to_all | solution.py:364
  67.4 0.0 copy-done
  67.4 0.0 copy-done.1
  67.4 2.7 %shard_map.97 = (f32[3,4096]{1,0:T(4,128)}, f32[1,1]{1,0:T(1,128)}) custom-call(s32[2,4096]{1,0:T(2,128)S(1)} %copy-done, s32[1,4096]{1,0:T(1,128)S(1)} %bitcast.12, f32[1,4096]{1,0:T(1,128)S(1)} %get-tuple-element.11.live_ref, f32[288,256]{1,0:T(8,128)S(1)} %get-tuple-element.12.slopes_ref, f32[16,4096]{1,0:T(8,128)S(1)} %get-tuple-element.13.owner_ref, ...), custom_call_target="tpu_custom_call" | custom-call | flops 3000000000 | bytes 10000000 | tf_op jit(solution)/shard_map/pallas_call | solution.py:352
Async XLA Ops:
  0.6 38.6 %copy-start.4 = (bf16[512,256]{1,0:T(8,128)(2,1)S(1)}, bf16[512,256]{1,0:T(8,128)(2,1)}, u32[]{:S(2)}) copy-start(bf16[512,256]{1,0:T(8,128)(2,1)} %constant.8.clone.order_ref) | copy-start | bytes 786436
  3.9 35.4 %copy-start.2 = (f32[514,256]{1,0:T(8,128)S(1)}, f32[514,256]{1,0:T(8,128)}, u32[]{:S(2)}) copy-start(f32[514,256]{1,0:T(8,128)} %constant.7.clone.plane_ref) | copy-start | bytes 1579012
  3.9 35.4 %copy-start.3 = (bf16[512,256]{1,0:T(8,128)(2,1)S(1)}, bf16[512,256]{1,0:T(8,128)(2,1)}, u32[]{:S(2)}) copy-start(bf16[512,256]{1,0:T(8,128)(2,1)} %constant.6.clone.table_hbm.table_ref) | copy-start | bytes 786436
  41.5 25.9 %copy-start = (s32[2,4096]{1,0:T(2,128)S(1)}, s32[2,4096]{1,0:T(2,128)}, u32[]{:S(2)}) copy-start(s32[2,4096]{1,0:T(2,128)} %offsets_ref.1) | copy-start | bytes 98308
  41.5 25.9 %copy-start.1 = (s32[4096]{0:T(1024)S(1)}, s32[4096]{0:T(1024)}, u32[]{:S(2)}) copy-start(s32[4096]{0:T(1024)} %param.9) | copy-start | bytes 49156

commit v8 on v7

--- a/solution.py
+++ b/solution.py
@@ -149,8 +149,8 @@
     slopes_ref, owner_ref, taps_z_ref, weight_x_ref, weight_y_ref, mesh_ref, packed_ref, counts_ref, offsets_ref, cell_z_ref, frac_ref, charges_ref, table_ref,
     sems,
 ):
-    sources = [counts_hbm, offsets_hbm, cell_z_hbm, frac_hbm, charges_hbm, table_hbm]
-    targets = [counts_ref, offsets_ref, cell_z_ref, frac_ref, charges_ref, table_ref]
+    sources = [frac_hbm, cell_z_hbm, offsets_hbm, charges_hbm, counts_hbm, table_hbm]
+    targets = [frac_ref, cell_z_ref, offsets_ref, charges_ref, counts_ref, table_ref]
     copies = [
         pltpu.make_async_copy(source, target, sems.at[i])
         for i, (source, target) in enumerate(zip(sources, targets))
@@ -158,8 +158,7 @@
     for copy in copies:
         copy.start()
     mesh_ref[...] = jnp.zeros_like(mesh_ref)
-    for copy in copies:
-        copy.wait()
+    copies[0].wait()
 
     def pack(first, end):
         for x in range(first, end):
@@ -174,6 +173,8 @@
     values, slopes = group_splines(frac_ref)
     for j in range(6):
         slopes_ref[48 * j : 48 * j + 48, :] = slopes[j]
+    for copy in copies[1:]:
+        copy.wait()
     for column in range(TILES_X):
         lanes, from_x, from_y, from_z = column_parts(column, offsets_ref, cell_z_ref)
         rows = [

time: 70.3 us -> 70.2 us (level)
  no operation moved by 1% of the time
where the time goes in v8:
time: 70.2 us; the launch traced here: 70 us
  blocking collectives  61.2 us (87%)
  Pallas kernels  8.08 us (12%)
    all_to_all x2, blocking collectives, exchange(): lax.all_to_all(block.reshape(256, 4, 128), AXES, 0, 0, tiled=True)  61.2 us
    pallas_call x3, Pallas kernels, call(): pl.pallas_call(kernel, out_shape=out_shape, in_specs=[pl.BlockSpec(memory...  8.08 us

profile of v8, /device:TPU:1, one launch (start us, length us, event | category | flops | bytes accessed | tf_op | source)
XLA Modules:
  0.0 70.0 jit_solution(1658511958475131148)
XLA Ops:
  0.6 0.0 copy-start.4
  0.6 3.1 %shard_map.95 = (f32[1024,128]{1,0:T(8,128)S(1)}, f32[1,4096]{1,0:T(1,128)S(1)}, f32[288,256]{1,0:T(8,128)S(1)}, f32[16,4096]{1,0:T(8,128)S(1)}, f32[16,4096]{1,...) custom-call(s32[64]{0:T(128)} %counts_hbm.1, s32[2,4096]{1,0:T(2,128)} %offsets_ref.1, s32[1,4096]{1,0:T(1,128)} %bitcast.11, ...), custom_call_target="tpu_custom_call" | custom-call | flops 3000000000 | bytes 10000000 | tf_op jit(solution)/shard_map/pallas_call | solution.py:353
  3.8 0.0 copy-start.2
  3.8 0.0 copy-start.3
  3.8 35.3 %all_to_all.10 = f32[256,4,128]{2,1,0:T(4,128)S(1)} all-to-all(f32[256,4,128]{2,1,0:T(4,128)S(1)} %bitcast.8), channel_id=1, replica_groups=mesh['grp'=8,'pen'=32] {'grp','pen'}, dimensions={0} | all-to-all | bytes 1048576 | tf_op jit(solution)/shard_map/all_to_all | solution.py:365
  39.1 0.0 copy-done.4
  39.1 0.0 copy-done.2
  39.1 0.0 copy-done.3
  39.2 2.2 %shard_map.96 = f32[1024,128]{1,0:T(8,128)S(1)} custom-call(f32[1024,128]{1,0:T(8,128)S(1)} %bitcast.9, f32[514,256]{1,0:T(8,128)S(1)} %copy-done.2, bf16[512,256]{1,0:T(8,128)(2,1)S(1)} %copy-done.4, bf16[512,256]{1,0:T(8,128)(2,1)S(1)} %copy-done.3), custom_call_target="tpu_custom_call" | custom-call | flops 3000000000 | bytes 10000000 | tf_op jit(solution)/shard_map/pallas_call | solution.py:353
  41.4 0.0 copy-start
  41.4 0.0 copy-start.1
  41.4 25.9 %all_to_all.11 = f32[256,4,128]{2,1,0:T(4,128)S(1)} all-to-all(f32[256,4,128]{2,1,0:T(4,128)S(1)} %bitcast.10), channel_id=1, replica_groups=mesh['grp'=8,'pen'=32] {'grp','pen'}, dimensions={0} | all-to-all | bytes 1048576 | tf_op jit(solution)/shard_map/all_to_all | solution.py:365
  67.3 0.0 copy-done
  67.3 0.0 copy-done.1
  67.3 2.7 %shard_map.97 = (f32[3,4096]{1,0:T(4,128)}, f32[1,1]{1,0:T(1,128)}) custom-call(s32[2,4096]{1,0:T(2,128)S(1)} %copy-done, s32[1,4096]{1,0:T(1,128)S(1)} %bitcast.12, f32[1,4096]{1,0:T(1,128)S(1)} %get-tuple-element.11.live_ref, f32[288,256]{1,0:T(8,128)S(1)} %get-tuple-element.12.slopes_ref, f32[16,4096]{1,0:T(8,128)S(1)} %get-tuple-element.13.owner_ref, ...), custom_call_target="tpu_custom_call" | custom-call | flops 3000000000 | bytes 10000000 | tf_op jit(solution)/shard_map/pallas_call | solution.py:353
Async XLA Ops:
  0.6 38.5 %copy-start.4 = (bf16[512,256]{1,0:T(8,128)(2,1)S(1)}, bf16[512,256]{1,0:T(8,128)(2,1)}, u32[]{:S(2)}) copy-start(bf16[512,256]{1,0:T(8,128)(2,1)} %constant.8.clone.order_ref) | copy-start | bytes 786436
  3.8 35.4 %copy-start.2 = (f32[514,256]{1,0:T(8,128)S(1)}, f32[514,256]{1,0:T(8,128)}, u32[]{:S(2)}) copy-start(f32[514,256]{1,0:T(8,128)} %constant.7.clone.plane_ref) | copy-start | bytes 1579012
  3.8 35.4 %copy-start.3 = (bf16[512,256]{1,0:T(8,128)(2,1)S(1)}, bf16[512,256]{1,0:T(8,128)(2,1)}, u32[]{:S(2)}) copy-start(bf16[512,256]{1,0:T(8,128)(2,1)} %constant.6.clone.table_hbm.table_ref) | copy-start | bytes 786436
  41.4 25.9 %copy-start = (s32[2,4096]{1,0:T(2,128)S(1)}, s32[2,4096]{1,0:T(2,128)}, u32[]{:S(2)}) copy-start(s32[2,4096]{1,0:T(2,128)} %offsets_ref.1) | copy-start | bytes 98308
  41.4 25.9 %copy-start.1 = (s32[4096]{0:T(1024)S(1)}, s32[4096]{0:T(1024)}, u32[]{:S(2)}) copy-start(s32[4096]{0:T(1024)} %param.9) | copy-start | bytes 49156

commit v9 on v8

--- a/solution.py
+++ b/solution.py
@@ -157,7 +157,6 @@
     ]
     for copy in copies:
         copy.start()
-    mesh_ref[...] = jnp.zeros_like(mesh_ref)
     copies[0].wait()
 
     def pack(first, end):
@@ -196,8 +195,12 @@
         weight_x_ref[:, lanes] = weight_x
         weight_y_ref[:, lanes] = weight_y
         weight_z = blocks_z(owner_z.astype(BF16), split(taps_z))
-        place = slice(32 * column, 32 * column + 112)
-        mesh_ref[place, :] += dot3(split(pair), weight_z, ((1,), (1,)))
+        part = dot3(split(pair), weight_z, ((1,), (1,)))
+        top = 32 * column
+        fresh = top + 80 if column else 0
+        if column:
+            mesh_ref[top:fresh, :] += part[:80, :]
+        mesh_ref[fresh : top + 112, :] = part[fresh - top :, :]
         if column == 9:
             pack(0, 20)
             transform(0)

time: 70.2 us -> 70.2 us (level)
  no operation moved by 1% of the time
where the time goes in v9:
time: 70.2 us; the launch traced here: 70 us
  blocking collectives  61.2 us (87%)
  Pallas kernels  8.09 us (12%)
    all_to_all x2, blocking collectives, exchange(): lax.all_to_all(block.reshape(256, 4, 128), AXES, 0, 0, tiled=True)  61.2 us
    pallas_call x3, Pallas kernels, call(): pl.pallas_call(kernel, out_shape=out_shape, in_specs=[pl.BlockSpec(memory...  8.09 us

profile of v9, /device:TPU:1, one launch (start us, length us, event | category | flops | bytes accessed | tf_op | source)
XLA Modules:
  0.0 70.0 jit_solution(13843346565875288960)
XLA Ops:
  0.6 0.0 copy-start.4
  0.6 3.1 %shard_map.95 = (f32[1024,128]{1,0:T(8,128)S(1)}, f32[1,4096]{1,0:T(1,128)S(1)}, f32[288,256]{1,0:T(8,128)S(1)}, f32[16,4096]{1,0:T(8,128)S(1)}, f32[16,4096]{1,...) custom-call(s32[64]{0:T(128)} %counts_hbm.1, s32[2,4096]{1,0:T(2,128)} %offsets_ref.1, s32[1,4096]{1,0:T(1,128)} %bitcast.11, ...), custom_call_target="tpu_custom_call" | custom-call | flops 3000000000 | bytes 10000000 | tf_op jit(solution)/shard_map/pallas_call | solution.py:356
  3.8 0.0 copy-start.2
  3.8 0.0 copy-start.3
  3.8 35.3 %all_to_all.10 = f32[256,4,128]{2,1,0:T(4,128)S(1)} all-to-all(f32[256,4,128]{2,1,0:T(4,128)S(1)} %bitcast.8), channel_id=1, replica_groups=mesh['grp'=8,'pen'=32] {'grp','pen'}, dimensions={0} | all-to-all | bytes 1048576 | tf_op jit(solution)/shard_map/all_to_all | solution.py:368
  39.1 0.0 copy-done.4
  39.1 0.0 copy-done.2
  39.2 0.0 copy-done.3
  39.2 2.2 %shard_map.96 = f32[1024,128]{1,0:T(8,128)S(1)} custom-call(f32[1024,128]{1,0:T(8,128)S(1)} %bitcast.9, f32[514,256]{1,0:T(8,128)S(1)} %copy-done.2, bf16[512,256]{1,0:T(8,128)(2,1)S(1)} %copy-done.4, bf16[512,256]{1,0:T(8,128)(2,1)S(1)} %copy-done.3), custom_call_target="tpu_custom_call" | custom-call | flops 3000000000 | bytes 10000000 | tf_op jit(solution)/shard_map/pallas_call | solution.py:356
  41.4 0.0 copy-start
  41.4 0.0 copy-start.1
  41.4 25.9 %all_to_all.11 = f32[256,4,128]{2,1,0:T(4,128)S(1)} all-to-all(f32[256,4,128]{2,1,0:T(4,128)S(1)} %bitcast.10), channel_id=1, replica_groups=mesh['grp'=8,'pen'=32] {'grp','pen'}, dimensions={0} | all-to-all | bytes 1048576 | tf_op jit(solution)/shard_map/all_to_all | solution.py:368
  67.3 0.0 copy-done
  67.3 0.0 copy-done.1
  67.3 2.7 %shard_map.97 = (f32[3,4096]{1,0:T(4,128)}, f32[1,1]{1,0:T(1,128)}) custom-call(s32[2,4096]{1,0:T(2,128)S(1)} %copy-done, s32[1,4096]{1,0:T(1,128)S(1)} %bitcast.12, f32[1,4096]{1,0:T(1,128)S(1)} %get-tuple-element.11.live_ref, f32[288,256]{1,0:T(8,128)S(1)} %get-tuple-element.12.slopes_ref, f32[16,4096]{1,0:T(8,128)S(1)} %get-tuple-element.13.owner_ref, ...), custom_call_target="tpu_custom_call" | custom-call | flops 3000000000 | bytes 10000000 | tf_op jit(solution)/shard_map/pallas_call | solution.py:356
Async XLA Ops:
  0.6 38.5 %copy-start.4 = (bf16[512,256]{1,0:T(8,128)(2,1)S(1)}, bf16[512,256]{1,0:T(8,128)(2,1)}, u32[]{:S(2)}) copy-start(bf16[512,256]{1,0:T(8,128)(2,1)} %constant.8.clone.order_ref) | copy-start | bytes 786436
  3.8 35.4 %copy-start.2 = (f32[514,256]{1,0:T(8,128)S(1)}, f32[514,256]{1,0:T(8,128)}, u32[]{:S(2)}) copy-start(f32[514,256]{1,0:T(8,128)} %constant.7.clone.plane_ref) | copy-start | bytes 1579012
  3.8 35.4 %copy-start.3 = (bf16[512,256]{1,0:T(8,128)(2,1)S(1)}, bf16[512,256]{1,0:T(8,128)(2,1)}, u32[]{:S(2)}) copy-start(bf16[512,256]{1,0:T(8,128)(2,1)} %constant.6.clone.table_hbm.table_ref) | copy-start | bytes 786436
  41.4 25.9 %copy-start = (s32[2,4096]{1,0:T(2,128)S(1)}, s32[2,4096]{1,0:T(2,128)}, u32[]{:S(2)}) copy-start(s32[2,4096]{1,0:T(2,128)} %offsets_ref.1) | copy-start | bytes 98308
  41.4 25.9 %copy-start.1 = (s32[4096]{0:T(1024)S(1)}, s32[4096]{0:T(1024)}, u32[]{:S(2)}) copy-start(s32[4096]{0:T(1024)} %param.9) | copy-start | bytes 49156
